TPU v7x, 32 devices: a whole 2x2x4 slice. The times are simulated.
32 devices in a mesh: hot: 4 (over z), cold: 8 (over y, x, core).
Axes of the slice: x: 2, y: 2, z: 4, core: 2. Of those that a mesh axis runs over, the one named last changes fastest.
Arguments:
- tokens: bfloat16 [128, 8192], P('cold', 'hot'), may hold values from -6 to 6
- hot_gate: bfloat16 [8192, 1024], P('hot', 'cold'), may hold values from -0.0625 to 0.0625
- hot_up: bfloat16 [8192, 1024], P('hot', 'cold'), may hold values from -0.0625 to 0.0625
- hot_down: bfloat16 [1024, 8192], P('cold', 'hot'), may hold values from -0.125 to 0.125
- cold_gate: bfloat16 [8192, 6144], P('hot', 'cold'), may hold values from -0.0625 to 0.0625
- cold_up: bfloat16 [8192, 6144], P('hot', 'cold'), may hold values from -0.0625 to 0.0625
- cold_down: bfloat16 [6144, 8192], P('cold', 'hot'), may hold values from -0.125 to 0.125
- hot_ids: int32 [8], replicated, may hold values from 0 to 55, as said below
- cold_ids: int32 [48], replicated, may hold values from 0 to 55, as said below
- block_mask: int32 [128, 56], replicated, may hold values from 0 to 1, as said below
Outputs:
- mixed: bfloat16 [128, 8192], P('cold', 'hot')
Inputs may be any that keep to these rules, and one draw needn't show every extreme that they name: hot_ids and cold_ids together name every block number from 0 to 55 once. `cold_ids`: cold slot s lies with index s // 6 of cold. `block_mask`: among the 16 tokens of one index of cold, at most 8 have a 1 in a cold slot of one given index of cold; in every draw some index of cold gets exactly 8 such tokens from every index of cold.
All inputs are finite; a program needn't handle non-finite values.
Results may differ from a plain program's by a relative error of at most 0.0049.
Values may be sent and summed in bfloat16 or wider, within the bound.
No kernel may reach another device: no remote copies, remote signals or barrier semaphores. Data moves between devices by JAX's collectives and lax.ppermute only.
A program may use at most 64 MiB of HBM per device.

v0:
```python
import jax
import jax.numpy as jnp
from jax import lax
from jax.sharding import PartitionSpec as P

BLOCK = 128


def expand_bits(block_bits):
    row_total = block_bits.shape[0]
    widened = jnp.broadcast_to(
        block_bits.astype(jnp.float32)[:, :, None], (row_total, block_bits.shape[1], BLOCK)
    )
    return widened.reshape(row_total, block_bits.shape[1] * BLOCK)


def gated_hidden(gate_sum, up_sum, block_bits):
    return (jax.nn.silu(gate_sum) * up_sum * expand_bits(block_bits)).astype(jnp.bfloat16)


def body(
    tokens, hot_gate, hot_up, hot_down, cold_gate, cold_up, cold_down, hot_ids, cold_ids, block_mask
):
    groups = lax.axis_size("cold")
    own_group = lax.axis_index("cold")
    local_rows = tokens.shape[0]
    slot_count = local_rows // 2
    all_rows = block_mask.shape[0]
    feature_cols = tokens.shape[1]
    hot_width = hot_gate.shape[1]
    hot_blocks = hot_width // BLOCK
    cold_blocks = cold_gate.shape[1] // BLOCK
    slot_rows = groups * slot_count
    cold_bits = jnp.take(block_mask, cold_ids, axis=1)
    group_hits = jnp.max(cold_bits.reshape(all_rows, groups, cold_blocks), axis=2)
    source_hits = group_hits.reshape(groups, local_rows, groups)
    slot_index = jnp.cumsum(source_hits, axis=1) - source_hits
    my_hits = lax.dynamic_index_in_dim(source_hits, own_group, 0, keepdims=False)
    my_slots = lax.dynamic_index_in_dim(slot_index, own_group, 0, keepdims=False)
    slot_range = jnp.arange(slot_count, dtype=jnp.int32)
    chosen = (my_slots.T[:, None, :] == slot_range[None, :, None]) & (my_hits.T[:, None, :] > 0)
    chosen = chosen.astype(jnp.bfloat16)
    outgoing = jnp.einsum("gst,td->gsd", chosen, tokens, preferred_element_type=jnp.float32).astype(
        jnp.bfloat16
    )
    arrived = lax.all_to_all(outgoing, "cold", split_axis=0, concat_axis=0, tiled=True)
    arrived = arrived.reshape(slot_rows, feature_cols)
    own_hits = lax.dynamic_index_in_dim(source_hits, own_group, 2, keepdims=False)
    own_slots = lax.dynamic_index_in_dim(slot_index, own_group, 2, keepdims=False)
    source_base = jnp.arange(groups, dtype=jnp.int32)[:, None] * slot_count
    target = jnp.where(own_hits > 0, source_base + own_slots, slot_rows).reshape(all_rows)
    row_token = (
        jnp.full((slot_rows + 1,), all_rows, jnp.int32)
        .at[target]
        .set(jnp.arange(all_rows, dtype=jnp.int32))[:slot_rows]
    )
    own_bits = lax.dynamic_slice_in_dim(cold_bits, own_group * cold_blocks, cold_blocks, 1)
    padded_bits = jnp.concatenate([own_bits, jnp.zeros((1, cold_blocks), own_bits.dtype)], axis=0)
    arrived_bits = jnp.take(padded_bits, row_token, axis=0)
    my_hot = lax.dynamic_slice_in_dim(hot_ids, own_group * hot_blocks, hot_blocks, 0)
    hot_bits = jnp.take(block_mask, my_hot, axis=1)
    both_hot = jnp.concatenate([hot_gate, hot_up], axis=1)
    hot_parts = jnp.dot(
        lax.all_gather(tokens, "cold", axis=0, tiled=True),
        both_hot,
        preferred_element_type=jnp.float32,
    )
    hot_gates = hot_parts[:, :hot_width]
    hot_ups = hot_parts[:, hot_width:]
    cold_gates = jnp.dot(arrived, cold_gate, preferred_element_type=jnp.float32)
    cold_ups = jnp.dot(arrived, cold_up, preferred_element_type=jnp.float32)
    hot_gates, hot_ups, cold_gates, cold_ups = lax.psum(
        (hot_gates, hot_ups, cold_gates, cold_ups), "hot"
    )
    hot_hidden = gated_hidden(hot_gates, hot_ups, hot_bits)
    cold_hidden = gated_hidden(cold_gates, cold_ups, arrived_bits)
    cold_out = jnp.dot(cold_hidden, cold_down, preferred_element_type=jnp.float32)
    returned = lax.all_to_all(
        cold_out.reshape(groups, slot_count, feature_cols),
        "cold",
        split_axis=0,
        concat_axis=0,
        tiled=True,
    )
    cold_mine = jnp.einsum(
        "gst,gsd->td", chosen.astype(jnp.float32), returned, precision=lax.Precision.HIGHEST
    )
    partial_value = jnp.dot(hot_hidden, hot_down, preferred_element_type=jnp.float32)
    combined = lax.psum_scatter(partial_value, "cold", scatter_dimension=0, tiled=True)
    combined = combined + cold_mine
    return combined.astype(jnp.bfloat16)


def solution(mesh):
    return jax.shard_map(
        body,
        mesh=mesh,
        in_specs=(
            P("cold", "hot"),
            P("hot", "cold"),
            P("hot", "cold"),
            P("cold", "hot"),
            P("hot", "cold"),
            P("hot", "cold"),
            P("cold", "hot"),
            P(),
            P(),
            P(),
        ),
        out_specs=P("cold", "hot"),
        check_vma=False,
    )
```

profile of v0, /device:TPU:0, one launch (start us, length us, event | category | flops | bytes accessed | tf_op | source)
XLA Modules:
  0.0 127.6 jit_solution(8542008087373703316)
XLA Ops:
  6.5 0.0 copy-start
  6.5 0.8 compare_select_fusion.2
  7.3 0.8 compare_and_fusion.1
  8.2 1.3 %gather_fusion = s32[48,128]{1,0:T(8,128)S(1)} fusion(s32[128,56]{0,1:T(8,128)} %param.19, s32[1024]{0:T(1024)S(1)} %pad_clamp_fusion.1), kind=kCustom, calls=%fused_computation | custom fusion | bytes 49344 | tf_op jit(solution)/shard_map/jit(_take)/gather | solution.py:34
  9.5 0.1 broadcast_in_dim.67
  9.6 0.1 select_reduce_fusion
  9.7 0.1 reshape.124
  9.8 0.1 copy.21
  9.9 0.7 reduce-window_subtract_fusion
  10.6 0.1 copy.23
  10.7 1.7 %convolution_convert_fusion = bf16[8,8,2048]{2,1,0:T(8,128)(2,1)} fusion(bf16[16,2048]{1,0:T(8,128)(2,1)} %param.10, s32[8,16]{1,0:T(8,128)S(1)} %bitcast.57, pred[8,16]{1,0:T(8,128)(4,1)S(1)} %bitcast.59), kind=kOutput, calls=%fused_computation.4 | convolution fusion | flops 4327424 | bytes 328320 | tf_op jit(solution)/shard_map/gst,td->gsd/dot_general | solution.py:43
  12.4 5.2 %all-to-all-start = ((bf16[8,8,2048]{2,1,0:T(8,128)(2,1)}), bf16[8,8,2048]{2,1,0:T(8,128)(2,1)S(1)}, u32[]{:S(2)}, u32[]{:S(2)}) async-start(bf16[8,8,2048]{2,1,0:T(8,128)(2,1)} %convolution_convert_fusion), calls=%async_computation.1 | async-start | bytes 524288 | tf_op jit(solution)/shard_map/all_to_all | solution.py:46
  17.6 0.0 all-reduce.4.cloned.1.call-start
  17.7 11.2 %all_gather.3 = bf16[128,2048]{1,0:T(8,128)(2,1)S(1)} all-gather(bf16[16,2048]{1,0:T(8,128)(2,1)} %param.10), channel_id=1, replica_groups=mesh['hot'=4,'cold'=8] {'cold'}, dimensions={0}, use_global_device_ids=true | all-gather | bytes 589824 | tf_op jit(solution)/shard_map/all_gather | solution.py:64
  28.9 1.2 dynamic_slice.20
  32.1 2.3 %convolution_bitcast_fusion.2 = f32[128,256]{0,1:T(8,128)} fusion(bf16[128,2048]{1,0:T(8,128)(2,1)S(1)} %all_gather.3, bf16[2048,128]{1,0:T(8,128)(2,1)} %param.12, bf16[2048,128]{1,0:T(8,128)(2,1)} %param.11), kind=kOutput, calls=%fused_computation.8 | convolution fusion | flops 136314880 | bytes 1703936 | tf_op jit(solution)/shard_map/dot_general | solution.py:63
  34.4 0.1 dynamic-slice.4
  34.5 1.5 %fusion.31 = (f32[128,128]{0,1:T(8,128)}, f32[128,128]{0,1:T(8,128)}) fusion(f32[128,256]{0,1:T(8,128)} %convolution_bitcast_fusion.2), kind=kLoop, calls=%fused_computation.57 | loop fusion | bytes 262144 | tf_op jit(solution)/shard_map/slice | solution.py:68
  36.0 0.0 all-to-all-done
  36.0 0.0 copy-start.1
  36.0 3.3 %fusion.5 = f32[64,768]{1,0:T(8,128)} fusion(bf16[2048,768]{1,0:T(8,128)(2,1)} %param.15, bf16[8,8,2048]{2,1,0:T(8,128)(2,1)S(1)} %all-to-all-done), kind=kOutput, calls=%fused_computation.13 | convolution fusion | flops 201326592 | bytes 3604480 | tf_op jit(solution)/shard_map/dot_general | solution.py:71
  39.4 0.0 copy-done.1
  39.4 1.3 %fusion.7 = f32[64,768]{1,0:T(8,128)} fusion(bf16[2048,768]{1,0:T(8,128)(2,1)S(1)} %copy-done.1, bf16[8,8,2048]{2,1,0:T(8,128)(2,1)S(1)} %all-to-all-done), kind=kOutput, calls=%fused_computation.15 | convolution fusion | flops 201326592 | bytes 3604480 | tf_op jit(solution)/shard_map/dot_general | solution.py:70
  40.7 0.0 all-reduce.4.cloned.1.call-update
  40.7 0.0 reduce-scatter.2.cloned.1.call-start
  40.7 0.7 fusion.24
  41.5 0.1 constant_dynamic-slice_fusion
  41.5 0.1 dynamic-slice_select_fusion
  41.6 38.2 %all-reduce.4.cloned.1.call-done = (f32[128,128]{0,1:T(8,128)}, f32[128,128]{0,1:T(8,128)}, f32[64,768]{1,0:T(8,128)}, f32[64,768]{1,0:T(8,128)}) async-done(((f32[128,128]{0,1:T(8,128)}, f32[128,128]{0,1:T(8,128)}, f32[64,768]{1,0:T(8,128)}, f32[64,768]{1,0:T(8,128)}), (f32[128,128]{0,1:T(8,128)}, f32[128,128]{0,1:T(8,128)}, f32[64,768]{1,0:T(8,128)}, f32[64,768]{1,0:T(8,128)})) %all-reduce.4.cloned.1.call-update) | async-done | bytes 524304 | tf_op jit(solution)/shard_map/psum | solution.py:72
  79.8 2.5 %fusion.13 = f32[128,2048]{1,0:T(8,128)} fusion(bf16[128,2048]{1,0:T(8,128)(2,1)} %param.13, f32[128,128]{0,1:T(8,128)} %get-tuple-element.16, f32[128,128]{0,1:T(8,128)} %get-tuple-element.17, f32[128]{0:T(128)S(1)} %fusion.24), kind=kOutput, calls=%fused_computation.22 | convolution fusion | flops 67223552 | bytes 1704448 | tf_op jit(solution)/shard_map/dot_general | solution.py:88
  82.3 0.0 reduce-scatter.2.cloned.1.call-update
  82.3 0.5 iota_multiply_fusion
  82.9 0.1 copy.27
  83.0 0.1 gt.38
  83.1 0.7 add.92
  83.8 0.1 add.93
  83.9 0.1 copy.24
  84.0 0.1 squeeze.11
  84.1 1.0 scatter_custom_fusion
  85.1 0.6 gather_fusion.1
  85.7 0.1 select_convert_fusion
  85.8 0.1 broadcast_in_dim.78
  85.9 0.0 copy-done
  85.9 0.0 copy-done.2
  85.9 1.6 %convolution_bitcast_fusion = f32[8,8,2048]{2,1,0:T(8,128)S(1)} fusion(bf16[768,2048]{1,0:T(8,128)(2,1)S(1)} %copy-done, f32[8,8,6,128]{3,2,1,0:T(8,128)S(1)} %bitcast.54, f32[64,768]{1,0:T(8,128)S(1)} %copy-done.2, f32[64,768]{1,0:T(8,128)} %get-tuple-element.19), kind=kOutput, calls=%fused_computation.3 | convolution fusion | flops 201670656 | bytes 4259840 | tf_op jit(solution)/shard_map/dot_general | solution.py:77
  87.5 13.1 %all_to_all.10 = f32[8,8,2048]{2,1,0:T(8,128)} all-to-all(f32[8,8,2048]{2,1,0:T(8,128)S(1)} %convolution_bitcast_fusion), channel_id=1, replica_groups=mesh['hot'=4,'cold'=8] {'cold'}, dimensions={0} | all-to-all | bytes 1048576 | tf_op jit(solution)/shard_map/all_to_all | solution.py:78
  100.6 18.2 %reduce-scatter.2.cloned.1.call-done = f32[16,2048]{1,0:T(8,128)} async-done(((f32[128,2048]{1,0:T(8,128)}), f32[16,2048]{1,0:T(8,128)}) %reduce-scatter.2.cloned.1.call-update) | async-done | bytes 131088 | tf_op jit(solution)/shard_map/reduce_scatter | solution.py:89
  118.8 2.0 %fusion.1 = bf16[16,2048]{1,0:T(8,128)(2,1)} fusion(f32[16,2048]{1,0:T(8,128)} %reduce-scatter.2.cloned.1.call-done, f32[8,8,2048]{2,1,0:T(8,128)} %all_to_all.10, s32[8,16]{1,0:T(8,128)S(1)} %bitcast.58, pred[8,16]{1,0:T(8,128)(4,1)S(1)} %bitcast.60), kind=kOutput, calls=%fused_computation.7 | convolution fusion | flops 25233408 | bytes 721536 | tf_op jit(solution)/shard_map/gst,gsd->td/dot_general | solution.py:85
  (12 shorter events, 0.1 us)
Async XLA Ops:
  6.5 79.4 %copy-start = (bf16[768,2048]{1,0:T(8,128)(2,1)S(1)}, bf16[768,2048]{1,0:T(8,128)(2,1)}, u32[]{:S(2)}) copy-start(bf16[768,2048]{1,0:T(8,128)(2,1)} %param.16) | copy-start | bytes 9437188
  12.4 23.6 %all-to-all-start = ((bf16[8,8,2048]{2,1,0:T(8,128)(2,1)}), bf16[8,8,2048]{2,1,0:T(8,128)(2,1)S(1)}, u32[]{:S(2)}, u32[]{:S(2)}) async-start(bf16[8,8,2048]{2,1,0:T(8,128)(2,1)} %convolution_convert_fusion), calls=%async_computation.1 | async-start | bytes 524288 | tf_op jit(solution)/shard_map/all_to_all | solution.py:46
  17.6 62.2 %all-reduce.4.cloned.1.call-start = ((), (), s32[]{:S(2)}) async-start(), calls=%async_computation.4 | async-start | bytes 1048576 | tf_op jit(solution)/shard_map/psum | solution.py:72
  36.0 3.3 %copy-start.1 = (bf16[2048,768]{1,0:T(8,128)(2,1)S(1)}, bf16[2048,768]{1,0:T(8,128)(2,1)}, u32[]{:S(2)}) copy-start(bf16[2048,768]{1,0:T(8,128)(2,1)} %param.14) | copy-start | bytes 9437188
  40.7 78.1 %reduce-scatter.2.cloned.1.call-start = ((), (), s32[]{:S(2)}) async-start(), calls=%async_computation.3 | async-start | bytes 1179648 | tf_op jit(solution)/shard_map/reduce_scatter | solution.py:89
  79.8 6.1 %copy-start.2 = (f32[64,768]{1,0:T(8,128)S(1)}, f32[64,768]{1,0:T(8,128)}, u32[]{:S(2)}) copy-start(f32[64,768]{1,0:T(8,128)} %get-tuple-element.18) | copy-start | bytes 589828
Sparse Core Ops, SparseCore 0:
  40.8 38.9 all-reduce.3
  83.0 35.7 reduce-scatter.1
where the time goes:
time: 128 us
  waiting for transfers between devices  56.4 us (44%)
  blocking collectives  24.3 us (19%)
  between operations  15.5 us (12%)
  matrix products  14.8 us (12%)
  local copies, waits for them, and re-layouts  7.53 us (6%)
  starting transfers between devices  5.28 us (4%)
  other arithmetic  3.81 us (3%)
    psum x1, waiting for transfers between devices, body(): lax.psum((hot_gates, hot_ups, cold_gates, cold_ups), 'hot')  38.2 us
    reduce_scatter x1, waiting for transfers between devices, body(): lax.psum_scatter(partial_value, 'cold', scatter_dimension=0, tiled=True)  18.2 us
    all_to_all x1, blocking collectives, body(): lax.all_to_all(cold_out.reshape(groups, slot_count, feature_cols), 'cold'...  13.1 us
    all_gather x1, blocking collectives, body(): lax.all_gather(tokens, 'cold', axis=0, tiled=True)  11.2 us
    all_to_all x1, starting transfers between devices, body(): lax.all_to_all(outgoing, 'cold', split_axis=0, concat_axis=0, tiled=True)  5.2 us
    dot_general x1, matrix products, body(): cold_ups = jnp.dot(arrived, cold_up, preferred_element_type=jnp.float32)  3.34 us
  transfers between devices with their start and end apart: 3, of which 2 were waited for; matrix products, arithmetic and copies ran while one was open for 9% of the time, Pallas kernels for 0%

commit v1 on v0

v1 whole, which is shorter than its diff:
```python
import functools

import jax
import jax.numpy as jnp
from jax import lax
from jax.experimental import pallas as pl
from jax.experimental.pallas import tpu as pltpu
from jax.sharding import PartitionSpec as P

BLOCK = 128
F32 = jnp.float32
BF16 = jnp.bfloat16
VM = pl.BlockSpec(memory_space=pltpu.VMEM)
SM = pl.BlockSpec(memory_space=pltpu.SMEM)
HB = pl.BlockSpec(memory_space=pl.ANY)


def params(mib):
    return pltpu.CompilerParams(vmem_limit_bytes=mib * 1024 * 1024)


def send(value, axis, size, mask):
    return lax.ppermute(value, axis, [(at, at ^ mask) for at in range(size)])


def route_kernel(place, ids, mask, pick, spread, row_bits, bits, ordered, *, order, rows, cold_blocks, hot_blocks):
    total, named = mask.shape
    own = place[0]
    groups = len(order)
    for at, mark in enumerate(order):
        first = pl.multiple_of((own ^ mark) * rows, rows)
        ordered[at * rows : (at + 1) * rows, :] = mask[pl.ds(first, rows), :]
    width = bits.shape[1]
    wanted = jnp.full((width, named), -1, jnp.int32)
    row = lax.broadcasted_iota(jnp.int32, (width, named), 0)
    for at in range(cold_blocks):
        wanted = jnp.where(row == at, ids[own * cold_blocks + at], wanted)
    for at in range(hot_blocks):
        hot_at = groups * cold_blocks + own * hot_blocks + at
        wanted = jnp.where(row == cold_blocks + at, ids[hot_at], wanted)
    column = lax.broadcasted_iota(jnp.int32, (width, named), 1)
    choose = (wanted == column).astype(F32).astype(BF16)
    active = ordered[...].astype(F32).astype(BF16)
    contract = (((1,), (1,)), ((), ()))
    by_token = lax.dot_general(active, choose, contract, preferred_element_type=F32)
    by_block = lax.dot_general(choose, active, contract, preferred_element_type=F32)
    bits[...] = by_token
    lane = lax.broadcasted_iota(jnp.int32, by_token.shape, 1)
    hit_col = jnp.max(jnp.where(lane < cold_blocks, by_token, 0.0), axis=1, keepdims=True)
    line = lax.broadcasted_iota(jnp.int32, by_block.shape, 0)
    hit_row = jnp.max(jnp.where(line < cold_blocks, by_block, 0.0), axis=0, keepdims=True)
    down = lax.broadcasted_iota(jnp.int32, (total, total), 0)
    across = lax.broadcasted_iota(jnp.int32, (total, total), 1)
    rank_col = jnp.sum(jnp.where(across < down, hit_row, 0.0), axis=1, keepdims=True)
    rank_row = jnp.sum(jnp.where(down < across, hit_col, 0.0), axis=0, keepdims=True)
    slot_row = jnp.where(hit_row > 0.0, rank_row, -1.0)
    slot_col = jnp.where(hit_col > 0.0, rank_col, -1.0)
    slots = total // 2
    chosen = lax.broadcasted_iota(jnp.int32, (slots, total), 0).astype(F32) == slot_row
    chosen = chosen.astype(F32).astype(BF16)
    pick[...] = chosen
    back = lax.broadcasted_iota(jnp.int32, (total, slots), 1).astype(F32) == slot_col
    spread[...] = back.astype(F32).astype(BF16)
    row_bits[...] = jnp.dot(chosen, by_token.astype(BF16), preferred_element_type=F32)


def chunk_of(width):
    return 256 if width % 256 == 0 else 128


def up_kernel(place, near, far, pick, hot_gate, hot_up, cold_gate, cold_up, *rest, parts):
    outs = rest[:parts]
    hot_gate_v, hot_up_v, cold_gate_v, cold_up_v, sums, sems = rest[parts:]
    cold_width = cold_gate.shape[1]
    hot_width = hot_gate.shape[1]
    step = chunk_of(cold_width)
    half = near.shape[0]
    gates = cold_width + 2 * hot_width
    moves = []
    for source, target in ((cold_gate, cold_gate_v), (cold_up, cold_up_v)):
        for at in range(0, cold_width, step):
            piece = pl.ds(at, step)
            moves.append((source.at[:, piece], target.at[:, piece]))
    moves.append((hot_gate, hot_gate_v))
    moves.append((hot_up, hot_up_v))
    copies = [pltpu.make_async_copy(a, b, sems.at[n]) for n, (a, b) in enumerate(moves)]
    for copy in copies:
        copy.start()
    near_rows = near[...]
    far_rows = far[...]
    picked = jnp.dot(pick[:, :half], near_rows, preferred_element_type=F32)
    picked = picked + jnp.dot(pick[:, half:], far_rows, preferred_element_type=F32)
    picked = picked.astype(BF16)
    at_copy = 0
    for base, target in ((0, cold_gate_v), (gates, cold_up_v)):
        for at in range(0, cold_width, step):
            copies[at_copy].wait()
            at_copy += 1
            value = jnp.dot(picked, target[:, at : at + step], preferred_element_type=F32)
            sums[:, base + at : base + at + step] = value.astype(BF16)
    for base, target in ((0, hot_gate_v), (gates, hot_up_v)):
        copies[at_copy].wait()
        at_copy += 1
        for side, rows in enumerate((near_rows, far_rows)):
            at = base + cold_width + side * hot_width
            value = jnp.dot(rows, target[...], preferred_element_type=F32)
            sums[:, at : at + hot_width] = value.astype(BF16)
    share = half // parts
    for mark, out in enumerate(outs):
        first = pl.multiple_of((place[1] ^ mark) * share, share)
        out[...] = sums[pl.ds(first, share), :]


def act_kernel(place, row_bits, bits, *rest, cold_blocks, hot_blocks):
    out = rest[-1]
    terms = rest[:-1]
    share = out.shape[0]
    gates = out.shape[1]
    slots = row_bits.shape[0]
    total = terms[0][...].astype(F32)
    for term in terms[1:]:
        total = total + term[...].astype(F32)
    first = pl.multiple_of(place[1] * share, share)
    cold_rows = row_bits[pl.ds(first, share), :]
    columns = [cold_rows[:, at : at + 1] for at in range(cold_blocks)]
    for side in range(2):
        begin = pl.multiple_of(side * slots + place[1] * share, share)
        hot_rows = bits[pl.ds(begin, share), :]
        columns += [hot_rows[:, cold_blocks + at : cold_blocks + at + 1] for at in range(hot_blocks)]
    for at, column in enumerate(columns):
        gate = total[:, at * BLOCK : (at + 1) * BLOCK]
        up = total[:, gates + at * BLOCK : gates + (at + 1) * BLOCK]
        value = gate / (1.0 + jnp.exp(-gate)) * up * column
        out[:, at * BLOCK : (at + 1) * BLOCK] = value.astype(BF16)


def down_kernel(place, spread, cold_down, hot_down, *rest, parts):
    blocks = rest[:parts]
    near, far, cold_v, hot_v, hidden, sems = rest[parts:]
    cold_width, features = cold_down.shape
    hot_width = hot_down.shape[0]
    step = chunk_of(features)
    copies = []
    for at in range(0, features, step):
        piece = pl.ds(at, step)
        slot = at // step
        copies.append(pltpu.make_async_copy(cold_down.at[:, piece], cold_v.at[:, piece], sems.at[0, slot]))
        copies.append(pltpu.make_async_copy(hot_down.at[:, piece], hot_v.at[:, piece], sems.at[1, slot]))
    for copy in copies:
        copy.start()
    share = blocks[0].shape[0]
    for mark, block in enumerate(blocks):
        first = pl.multiple_of((place[1] ^ mark) * share, share)
        hidden[pl.ds(first, share), :] = block[...]
    half = near.shape[0]
    cold_rows = jnp.dot(spread[...], hidden[:, :cold_width], preferred_element_type=F32).astype(BF16)
    hot_near = hidden[:, cold_width : cold_width + hot_width]
    hot_far = hidden[:, cold_width + hot_width :]
    hot_rows = jnp.concatenate([hot_near, hot_far], axis=0)
    for at in range(0, features, step):
        copies[2 * (at // step)].wait()
        copies[2 * (at // step) + 1].wait()
        value = jnp.dot(cold_rows, cold_v[:, at : at + step], preferred_element_type=F32)
        value = value + jnp.dot(hot_rows, hot_v[:, at : at + step], preferred_element_type=F32)
        value = value.astype(BF16)
        near[:, at : at + step] = value[:half]
        far[:, at : at + step] = value[half:]


def body(
    tokens, hot_gate, hot_up, hot_down, cold_gate, cold_up, cold_down, hot_ids, cold_ids, block_mask
):
    groups = lax.axis_size("cold")
    ranges = lax.axis_size("hot")
    place = jnp.stack([lax.axis_index("cold"), lax.axis_index("hot")]).astype(jnp.int32)
    rows, features = tokens.shape
    total, named = block_mask.shape
    half = total // 2
    share = half // ranges
    hot_width = hot_gate.shape[1]
    cold_width = cold_gate.shape[1]
    hot_blocks = hot_width // BLOCK
    cold_blocks = cold_width // BLOCK
    gates = cold_width + 2 * hot_width
    order = list(range(0, groups, 2)) + list(range(1, groups, 2))
    bits_width = -(-(cold_blocks + hot_blocks) // 8) * 8

    near = [tokens] + [send(tokens, "cold", groups, mark) for mark in range(2, groups, 2)]
    near = jnp.concatenate(near, axis=0)
    far = send(near, "cold", groups, 1)

    ids = jnp.concatenate([cold_ids, hot_ids])
    pick, spread, row_bits, bits = pl.pallas_call(
        functools.partial(
            route_kernel, order=order, rows=rows, cold_blocks=cold_blocks, hot_blocks=hot_blocks
        ),
        out_shape=(
            jax.ShapeDtypeStruct((half, total), BF16),
            jax.ShapeDtypeStruct((total, half), BF16),
            jax.ShapeDtypeStruct((half, bits_width), F32),
            jax.ShapeDtypeStruct((total, bits_width), F32),
        ),
        in_specs=[SM, SM, VM],
        out_specs=(VM, VM, VM, VM),
        scratch_shapes=[pltpu.VMEM((total, named), jnp.int32)],
        compiler_params=params(16),
        name="route",
    )(place, ids, block_mask)

    copies = 2 * (cold_width // chunk_of(cold_width)) + 2
    partial_sums = pl.pallas_call(
        functools.partial(up_kernel, parts=ranges),
        out_shape=tuple(jax.ShapeDtypeStruct((share, 2 * gates), BF16) for _ in range(ranges)),
        in_specs=[SM, VM, VM, VM, HB, HB, HB, HB],
        out_specs=tuple(VM for _ in range(ranges)),
        scratch_shapes=[
            pltpu.VMEM((features, hot_width), BF16),
            pltpu.VMEM((features, hot_width), BF16),
            pltpu.VMEM((features, cold_width), BF16),
            pltpu.VMEM((features, cold_width), BF16),
            pltpu.VMEM((half, 2 * gates), BF16),
            pltpu.SemaphoreType.DMA((copies,)),
        ],
        compiler_params=params(24),
        name="up",
    )(place, near, far, pick, hot_gate, hot_up, cold_gate, cold_up)

    terms = [partial_sums[0]]
    terms += [send(partial_sums[mark], "hot", ranges, mark) for mark in range(1, ranges)]
    own_hidden = pl.pallas_call(
        functools.partial(act_kernel, cold_blocks=cold_blocks, hot_blocks=hot_blocks),
        out_shape=jax.ShapeDtypeStruct((share, gates), BF16),
        in_specs=[SM, VM, VM] + [VM] * ranges,
        out_specs=VM,
        compiler_params=params(16),
        name="act",
    )(place, row_bits, bits, *terms)

    blocks = [own_hidden] + [send(own_hidden, "hot", ranges, mark) for mark in range(1, ranges)]
    near_out, far_out = pl.pallas_call(
        functools.partial(down_kernel, parts=ranges),
        out_shape=(
            jax.ShapeDtypeStruct((half, features), BF16),
            jax.ShapeDtypeStruct((half, features), BF16),
        ),
        in_specs=[SM, VM, HB, HB] + [VM] * ranges,
        out_specs=(VM, VM),
        scratch_shapes=[
            pltpu.VMEM((cold_width, features), BF16),
            pltpu.VMEM((hot_width, features), BF16),
            pltpu.VMEM((half, gates), BF16),
            pltpu.SemaphoreType.DMA((2, features // chunk_of(features))),
        ],
        compiler_params=params(24),
        name="down",
    )(place, spread, cold_down, hot_down, *blocks)

    pair = near_out.astype(F32) + send(far_out, "cold", groups, 1).astype(F32)
    result = pair[:rows]
    for at in range(1, groups // 2):
        piece = pair[at * rows : (at + 1) * rows].astype(BF16)
        result = result + send(piece, "cold", groups, 2 * at).astype(F32)
    return result.astype(BF16)


def solution(mesh):
    return jax.shard_map(
        body,
        mesh=mesh,
        in_specs=(
            P("cold", "hot"),
            P("hot", "cold"),
            P("hot", "cold"),
            P("cold", "hot"),
            P("hot", "cold"),
            P("hot", "cold"),
            P("cold", "hot"),
            P(),
            P(),
            P(),
        ),
        out_specs=P("cold", "hot"),
        check_vma=False,
    )
```

time: 128 us -> 54.6 us (0.43)
  waiting for transfers between devices: 56.4 us -> 18.2 us
  blocking collectives: 24.3 us -> 0 us
  between operations: 15.5 us -> 0.1 us
  matrix products: 14.8 us -> 0 us
  starting transfers between devices: 5.28 us -> 17 us
  Pallas kernels: 0 us -> 9.69 us
  other arithmetic: 3.81 us -> 1.55 us
    psum x1 -> x0, waiting for transfers between devices: 38.2 us -> none  [body(): lax.psum((hot_gates, hot_ups, cold_gates, cold_ups), 'hot')]
    ppermute x0 -> x14, waiting for transfers between devices: none -> 18.2 us  [send(): return lax.ppermute(value, axis, [(at, at ^ mask) for at in range(size)])]
    reduce_scatter x1 -> x0, waiting for transfers between devices: 18.2 us -> none  [body(): lax.psum_scatter(partial_value, 'cold', scatter_dimension=0, tiled=True)]
    ppermute x0 -> x14, starting transfers between devices: none -> 17 us  [send(): return lax.ppermute(value, axis, [(at, at ^ mask) for at in range(size)])]
    dot_general x7 -> x0, matrix products: 14.8 us -> none  [the longest x1 3.34 us: body(): cold_ups = jnp.dot(arrived, cold_up, preferred_element_type=jnp.float32)]
    all_to_all x1 -> x0, blocking collectives: 13.1 us -> none  [body(): lax.all_to_all(cold_out.reshape(groups, slot_count, feature_cols), 'cold'...]
    all_gather x1 -> x0, blocking collectives: 11.2 us -> none  [body(): lax.all_gather(tokens, 'cold', axis=0, tiled=True)]
    pallas_call x0 -> x4, Pallas kernels: none -> 9.69 us  [the longest x1 4.59 us: body(): pl.pallas_call(functools.partial(up_kernel, parts=ranges), out_shape=tupl...]
  transfers between devices with their start and end apart: 3 -> 14, of which waited for: 2 -> 11; matrix products, arithmetic and copies ran while one was open for 9% -> 5% of each run, Pallas kernels for 0% -> 2%
where the time goes in v1:
time: 54.6 us; the launch traced here: 54.2 us
  waiting for transfers between devices  18.2 us (33%)
  starting transfers between devices  17 us (31%)
  Pallas kernels  9.69 us (18%)
  local copies, waits for them, and re-layouts  7.65 us (14%)
  other arithmetic  1.55 us (3%)
    ppermute x14, waiting for transfers between devices, send(): return lax.ppermute(value, axis, [(at, at ^ mask) for at in range(size)])  18.2 us
    ppermute x14, starting transfers between devices, send(): return lax.ppermute(value, axis, [(at, at ^ mask) for at in range(size)])  17 us
    unnamed x16, local copies, waits for them, and re-layouts  7.63 us
    pallas_call x1, Pallas kernels, body(): pl.pallas_call(functools.partial(up_kernel, parts=ranges), out_shape=tupl...  4.59 us
    pallas_call x1, Pallas kernels, body(): pl.pallas_call(functools.partial(down_kernel, parts=ranges), out_shape=(j...  3.57 us
  transfers between devices with their start and end apart: 14, of which 11 were waited for; matrix products, arithmetic and copies ran while one was open for 5% of the time, Pallas kernels for 2%

profile of v1, /device:TPU:0, one launch (start us, length us, event | category | flops | bytes accessed | tf_op | source)
XLA Modules:
  0.0 54.2 jit_solution(18358796450646970956)
XLA Ops:
  0.0 3.0 %collective-permute-start.1 = (bf16[16,2048]{1,0:T(8,128)(2,1)}, bf16[16,2048]{1,0:T(8,128)(2,1)S(1)}, u32[]{:S(2)}, u32[]{:S(2)}) collective-permute-start(bf16[16,2048]{1,0:T(8,128)(2,1)} %param.10), channel_id=1, source_target_pairs={{0,4},{1,5},{2,6},{3,7},{4,0},{5,1},{6,2},{7,3},{8,12},{9,13},{10,... | collective-permute-start | bytes 196616 | tf_op jit(solution)/shard_map/ppermute | solution.py:23
  3.0 1.5 %collective-permute-start = (bf16[16,2048]{1,0:T(8,128)(2,1)}, bf16[16,2048]{1,0:T(8,128)(2,1)S(1)}, u32[]{:S(2)}, u32[]{:S(2)}) collective-permute-start(bf16[16,2048]{1,0:T(8,128)(2,1)} %param.10), channel_id=1, source_target_pairs={{0,2},{1,3},{2,0},{3,1},{4,6},{5,7},{6,4},{7,5},{8,10},{9,11},{10,... | collective-permute-start | bytes 196616 | tf_op jit(solution)/shard_map/ppermute | solution.py:23
  4.5 0.0 collective-permute-start.2
  4.5 0.9 %constant_dynamic-update-slice_fusion.3 = bf16[64,2048]{1,0:T(8,128)(2,1)S(1)} fusion(bf16[16,2048]{1,0:T(8,128)(2,1)} %param.10), kind=kLoop, calls=%fused_computation.8 | loop fusion | bytes 131072
  5.4 2.5 %collective-permute-done = bf16[16,2048]{1,0:T(8,128)(2,1)S(1)} collective-permute-done((bf16[16,2048]{1,0:T(8,128)(2,1)}, bf16[16,2048]{1,0:T(8,128)(2,1)S(1)}, u32[]{:S(2)}, u32[]{:S(2)}) %collective-permute-start) | collective-permute-done | bytes 65568 | tf_op jit(solution)/shard_map/ppermute | solution.py:23
  7.9 0.0 collective-permute-done.1
  7.9 1.9 %collective-permute-done.2 = bf16[16,2048]{1,0:T(8,128)(2,1)S(1)} collective-permute-done((bf16[16,2048]{1,0:T(8,128)(2,1)}, bf16[16,2048]{1,0:T(8,128)(2,1)S(1)}, u32[]{:S(2)}, u32[]{:S(2)}) %collective-permute-start.2) | collective-permute-done | bytes 65568 | tf_op jit(solution)/shard_map/ppermute | solution.py:23
  9.9 0.0 collective-permute-start.3
  9.9 0.8 %copy.11.mask = s32[128,56]{1,0:T(8,128)S(1)} copy(s32[128,56]{0,1:T(8,128)} %param.19) | data formatting | bytes 57344 | tf_op args[9]
  10.7 0.1 pad_add_fusion.place
  10.8 0.7 %pad_add_fusion.1.ids = s32[56]{0:T(128)S(1)} fusion(s32[8]{0:T(128)} %param.17, s32[48]{0:T(128)} %param.18), kind=kLoop, calls=%fused_computation.10 | loop fusion | flops 56 | bytes 448 | tf_op jit(solution)/shard_map/concatenate | solution.py:192
  11.6 0.9 %route.1 = (bf16[64,128]{1,0:T(8,128)(2,1)S(1)}, bf16[128,64]{1,0:T(8,128)(2,1)S(1)}, f32[64,8]{1,0:T(8,128)S(1)}, f32[128,8]{1,0:T(8,128)S(1)}) custom-call(s32[2]{0:T(128)S(1)} %pad_add_fusion.place, s32[56]{0:T(128)S(1)} %pad_add_fusion.1.ids, s32[128,56]{1,0:T(8,128)S(1)} %copy.11.mask), custom_call_target="tpu_custom_call" | custom-call | tf_op jit(solution)/shard_map/route/pallas_call | solution.py:193
  12.5 0.0 collective-permute-done.3.far
  12.5 0.0 copy-start.1
  12.5 1.9 %copy-done.1 = bf16[2048,768]{1,0:T(8,128)(2,1)S(1)} copy-done((bf16[2048,768]{1,0:T(8,128)(2,1)S(1)}, bf16[2048,768]{1,0:T(8,128)(2,1)}, u32[]{:S(2)}) %copy-start.1) | copy-done | bytes 3145752
  14.4 0.0 copy-start.2
  14.4 1.9 %copy-done.2 = bf16[2048,768]{1,0:T(8,128)(2,1)S(1)} copy-done((bf16[2048,768]{1,0:T(8,128)(2,1)S(1)}, bf16[2048,768]{1,0:T(8,128)(2,1)}, u32[]{:S(2)}) %copy-start.2) | copy-done | bytes 3145752
  16.2 0.0 copy-start.3
  16.2 1.0 %copy-done.3 = bf16[2048,128]{1,0:T(8,128)(2,1)S(1)} copy-done((bf16[2048,128]{1,0:T(8,128)(2,1)S(1)}, bf16[2048,128]{1,0:T(8,128)(2,1)}, u32[]{:S(2)}) %copy-start.3) | copy-done | bytes 524312
  17.3 0.0 copy-start.4
  17.3 1.0 %copy-done.4 = bf16[2048,128]{1,0:T(8,128)(2,1)S(1)} copy-done((bf16[2048,128]{1,0:T(8,128)(2,1)S(1)}, bf16[2048,128]{1,0:T(8,128)(2,1)}, u32[]{:S(2)}) %copy-start.4) | copy-done | bytes 524312
  18.3 4.6 %up.1 = (bf16[16,2048]{1,0:T(8,128)(2,1)S(1)}, bf16[16,2048]{1,0:T(8,128)(2,1)S(1)}, bf16[16,2048]{1,0:T(8,128)(2,1)S(1)}, bf16[16,2048]{1,0:T(8,128)(2,1)S(1)}) custom-call(s32[2]{0:T(128)S(1)} %pad_add_fusion.place, bf16[64,2048]{1,0:T(8,128)(2,1)S(1)} %constant_dynamic-update-slice_fusion.near, bf16[64,2048]{1,0:T(8,128)(2,1)S(1)} %collective-permute-done.3.far, ...), custom_call_target="tpu_custom_call" | custom-call | tf_op jit(solution)/shard_map/up/pallas_call | solution.py:211
  22.9 1.6 %collective-permute-start.4 = (bf16[16,2048]{1,0:T(8,128)(2,1)S(1)}, bf16[16,2048]{1,0:T(8,128)(2,1)S(1)}, u32[]{:S(2)}, u32[]{:S(2)}) collective-permute-start(bf16[16,2048]{1,0:T(8,128)(2,1)S(1)} %get-tuple-element.20), channel_id=1, source_target_pairs={{0,8},{8,0},{16,24},{24,16},{1,9},{9,1},{17,25},{25,17},{2,10},{10... | collective-permute-start | bytes 196616 | tf_op jit(solution)/shard_map/ppermute | solution.py:23
  24.6 2.6 %collective-permute-start.5 = (bf16[16,2048]{1,0:T(8,128)(2,1)S(1)}, bf16[16,2048]{1,0:T(8,128)(2,1)S(1)}, u32[]{:S(2)}, u32[]{:S(2)}) collective-permute-start(bf16[16,2048]{1,0:T(8,128)(2,1)S(1)} %get-tuple-element.21), channel_id=1, source_target_pairs={{0,16},{8,24},{16,0},{24,8},{1,17},{9,25},{17,1},{25,9},{2,18},{10... | collective-permute-start | bytes 196616 | tf_op jit(solution)/shard_map/ppermute | solution.py:23
  27.2 0.2 collective-permute-start.6
  27.4 0.1 collective-permute-done.4.rest_1_
  27.5 4.1 %collective-permute-done.5.rest_2_ = bf16[16,2048]{1,0:T(8,128)(2,1)S(1)} collective-permute-done((bf16[16,2048]{1,0:T(8,128)(2,1)S(1)}, bf16[16,2048]{1,0:T(8,128)(2,1)S(1)}, u32[]{:S(2)}, u32[]{:S(2)}) %collective-permute-start.5) | collective-permute-done | bytes 65568 | tf_op jit(solution)/shard_map/ppermute | solution.py:23
  31.6 1.6 %collective-permute-done.6.rest_3_ = bf16[16,2048]{1,0:T(8,128)(2,1)S(1)} collective-permute-done((bf16[16,2048]{1,0:T(8,128)(2,1)S(1)}, bf16[16,2048]{1,0:T(8,128)(2,1)S(1)}, u32[]{:S(2)}, u32[]{:S(2)}) %collective-permute-start.6) | collective-permute-done | bytes 65568 | tf_op jit(solution)/shard_map/ppermute | solution.py:23
  33.2 0.6 %act.1.rest_0_ = bf16[16,1024]{1,0:T(8,128)(2,1)S(1)} custom-call(s32[2]{0:T(128)S(1)} %pad_add_fusion.place, f32[64,8]{1,0:T(8,128)S(1)} %get-tuple-element.16.row_bits, f32[128,8]{1,0:T(8,128)S(1)} %get-tuple-element.17.bits, bf16[16,2048]{1,0:T(8,128)(2,1)S(1)} %get-tuple-element.19.rest_0_, bf16[16,2048]{1,0:T(8,128)(2,1)S(1)} %collective-permute-done.4.rest_1_, ...), custom_call_target="tpu_custom_call" | custom-call | tf_op jit(solution)/shard_map/act/pallas_call | solution.py:230
  33.9 2.5 %collective-permute-start.9 = (bf16[16,1024]{1,0:T(8,128)(2,1)S(1)}, bf16[16,1024]{1,0:T(8,128)(2,1)S(1)}, u32[]{:S(2)}, u32[]{:S(2)}) collective-permute-start(bf16[16,1024]{1,0:T(8,128)(2,1)S(1)} %act.1.rest_0_), channel_id=1, source_target_pairs={{0,24},{8,16},{16,8},{24,0},{1,25},{9,17},{17,9},{25,1},{2,26},{10... | collective-permute-start | bytes 98312 | tf_op jit(solution)/shard_map/ppermute | solution.py:23
  36.4 0.3 collective-permute-start.8
  36.7 1.6 %collective-permute-start.7 = (bf16[16,1024]{1,0:T(8,128)(2,1)S(1)}, bf16[16,1024]{1,0:T(8,128)(2,1)S(1)}, u32[]{:S(2)}, u32[]{:S(2)}) collective-permute-start(bf16[16,1024]{1,0:T(8,128)(2,1)S(1)} %act.1.rest_0_), channel_id=1, source_target_pairs={{0,8},{8,0},{16,24},{24,16},{1,9},{9,1},{17,25},{25,17},{2,10},{10... | collective-permute-start | bytes 98312 | tf_op jit(solution)/shard_map/ppermute | solution.py:23
  38.3 1.3 %collective-permute-done.9.rest_3_ = bf16[16,1024]{1,0:T(8,128)(2,1)S(1)} collective-permute-done((bf16[16,1024]{1,0:T(8,128)(2,1)S(1)}, bf16[16,1024]{1,0:T(8,128)(2,1)S(1)}, u32[]{:S(2)}, u32[]{:S(2)}) %collective-permute-start.9) | collective-permute-done | bytes 32800 | tf_op jit(solution)/shard_map/ppermute | solution.py:23
  39.7 1.7 %collective-permute-done.8.rest_2_ = bf16[16,1024]{1,0:T(8,128)(2,1)S(1)} collective-permute-done((bf16[16,1024]{1,0:T(8,128)(2,1)S(1)}, bf16[16,1024]{1,0:T(8,128)(2,1)S(1)}, u32[]{:S(2)}, u32[]{:S(2)}) %collective-permute-start.8) | collective-permute-done | bytes 32800 | tf_op jit(solution)/shard_map/ppermute | solution.py:23
  41.3 0.0 collective-permute-done.7.rest_1_
  41.3 0.0 copy-done
  41.3 0.0 copy-done.5
  41.4 3.6 %down.1 = (bf16[64,2048]{1,0:T(8,128)(2,1)S(1)}, bf16[64,2048]{1,0:T(8,128)(2,1)S(1)}) custom-call(s32[2]{0:T(128)S(1)} %pad_add_fusion.place, bf16[128,64]{1,0:T(8,128)(2,1)S(1)} %get-tuple-element.15.spread, bf16[768,2048]{1,0:T(8,128)(2,1)S(1)} %copy-done, bf16[128,2048]{1,0:T(8,128)(2,1)S(1)} %copy-done.5, bf16[16,1024]{1,0:T(8,128)(2,1)S(1)} %act.1.rest_0_, ...), custom_call_target="tpu_custom_call" | custom-call | tf_op jit(solution)/shard_map/down/pallas_call | solution.py:240
  44.9 0.1 collective-permute-start.10
  45.0 1.5 %collective-permute-done.10 = bf16[64,2048]{1,0:T(8,128)(2,1)S(1)} collective-permute-done((bf16[64,2048]{1,0:T(8,128)(2,1)S(1)}, bf16[64,2048]{1,0:T(8,128)(2,1)S(1)}, u32[]{:S(2)}, u32[]{:S(2)}) %collective-permute-start.10) | collective-permute-done | bytes 262176 | tf_op jit(solution)/shard_map/ppermute | solution.py:23
  46.5 0.1 fusion.3
  46.6 0.6 %collective-permute-start.11 = (bf16[16,2048]{1,0:T(8,128)(2,1)S(1)}, bf16[16,2048]{1,0:T(8,128)(2,1)S(1)}, u32[]{:S(2)}, u32[]{:S(2)}) collective-permute-start(bf16[16,2048]{1,0:T(8,128)(2,1)S(1)} %get-tuple-element.27), channel_id=1, source_target_pairs={{0,2},{1,3},{2,0},{3,1},{4,6},{5,7},{6,4},{7,5},{8,10},{9,11},{10,... | collective-permute-start | bytes 196616 | tf_op jit(solution)/shard_map/ppermute | solution.py:23
  47.2 1.4 %collective-permute-start.13 = (bf16[16,2048]{1,0:T(8,128)(2,1)S(1)}, bf16[16,2048]{1,0:T(8,128)(2,1)S(1)}, u32[]{:S(2)}, u32[]{:S(2)}) collective-permute-start(bf16[16,2048]{1,0:T(8,128)(2,1)S(1)} %get-tuple-element.28), channel_id=1, source_target_pairs={{0,6},{1,7},{2,4},{3,5},{4,2},{5,3},{6,0},{7,1},{8,14},{9,15},{10,... | collective-permute-start | bytes 196616 | tf_op jit(solution)/shard_map/ppermute | solution.py:23
  48.7 1.5 %collective-permute-start.12 = (bf16[16,2048]{1,0:T(8,128)(2,1)S(1)}, bf16[16,2048]{1,0:T(8,128)(2,1)S(1)}, u32[]{:S(2)}, u32[]{:S(2)}) collective-permute-start(bf16[16,2048]{1,0:T(8,128)(2,1)S(1)} %get-tuple-element.29), channel_id=1, source_target_pairs={{0,4},{1,5},{2,6},{3,7},{4,0},{5,1},{6,2},{7,3},{8,12},{9,13},{10,... | collective-permute-start | bytes 196616 | tf_op jit(solution)/shard_map/ppermute | solution.py:23
  50.2 1.3 %collective-permute-done.11 = bf16[16,2048]{1,0:T(8,128)(2,1)S(1)} collective-permute-done((bf16[16,2048]{1,0:T(8,128)(2,1)S(1)}, bf16[16,2048]{1,0:T(8,128)(2,1)S(1)}, u32[]{:S(2)}, u32[]{:S(2)}) %collective-permute-start.11) | collective-permute-done | bytes 65568 | tf_op jit(solution)/shard_map/ppermute | solution.py:23
  51.5 0.9 %collective-permute-done.13 = bf16[16,2048]{1,0:T(8,128)(2,1)S(1)} collective-permute-done((bf16[16,2048]{1,0:T(8,128)(2,1)S(1)}, bf16[16,2048]{1,0:T(8,128)(2,1)S(1)}, u32[]{:S(2)}, u32[]{:S(2)}) %collective-permute-start.13) | collective-permute-done | bytes 65568 | tf_op jit(solution)/shard_map/ppermute | solution.py:23
  52.4 1.1 %collective-permute-done.12 = bf16[16,2048]{1,0:T(8,128)(2,1)S(1)} collective-permute-done((bf16[16,2048]{1,0:T(8,128)(2,1)S(1)}, bf16[16,2048]{1,0:T(8,128)(2,1)S(1)}, u32[]{:S(2)}, u32[]{:S(2)}) %collective-permute-start.12) | collective-permute-done | bytes 65568 | tf_op jit(solution)/shard_map/ppermute | solution.py:23
  53.5 0.7 %fusion.2 = bf16[16,2048]{1,0:T(8,128)(2,1)} fusion(f32[64,2048]{1,0:T(8,128)S(1)} %get-tuple-element.26, bf16[16,2048]{1,0:T(8,128)(2,1)S(1)} %collective-permute-done.13, bf16[16,2048]{1,0:T(8,128)(2,1)S(1)} %collective-permute-done.12, bf16[16,2048]{1,0:T(8,128)(2,1)S(1)} %collective-permute-done.11), kind=kLoop, calls=%fused_computation.4 | loop fusion | flops 229376 | bytes 393216 | tf_op jit(solution)/shard_map/convert_element_type | solution.py:263
  (6 shorter events, 0.0 us)
Async XLA Ops:
  0.0 7.9 %collective-permute-start.1 = (bf16[16,2048]{1,0:T(8,128)(2,1)}, bf16[16,2048]{1,0:T(8,128)(2,1)S(1)}, u32[]{:S(2)}, u32[]{:S(2)}) collective-permute-start(bf16[16,2048]{1,0:T(8,128)(2,1)} %param.10), channel_id=1, source_target_pairs={{0,4},{1,5},{2,6},{3,7},{4,0},{5,1},{6,2},{7,3},{8,12},{9,13},{10,... | collective-permute-start | bytes 196616 | tf_op jit(solution)/shard_map/ppermute | solution.py:23
  3.0 4.9 %collective-permute-start = (bf16[16,2048]{1,0:T(8,128)(2,1)}, bf16[16,2048]{1,0:T(8,128)(2,1)S(1)}, u32[]{:S(2)}, u32[]{:S(2)}) collective-permute-start(bf16[16,2048]{1,0:T(8,128)(2,1)} %param.10), channel_id=1, source_target_pairs={{0,2},{1,3},{2,0},{3,1},{4,6},{5,7},{6,4},{7,5},{8,10},{9,11},{10,... | collective-permute-start | bytes 196616 | tf_op jit(solution)/shard_map/ppermute | solution.py:23
  4.5 5.4 %collective-permute-start.2 = (bf16[16,2048]{1,0:T(8,128)(2,1)}, bf16[16,2048]{1,0:T(8,128)(2,1)S(1)}, u32[]{:S(2)}, u32[]{:S(2)}) collective-permute-start(bf16[16,2048]{1,0:T(8,128)(2,1)} %param.10), channel_id=1, source_target_pairs={{0,6},{1,7},{2,4},{3,5},{4,2},{5,3},{6,0},{7,1},{8,14},{9,15},{10,... | collective-permute-start | bytes 196616 | tf_op jit(solution)/shard_map/ppermute | solution.py:23
  9.9 2.6 %collective-permute-start.3 = (bf16[64,2048]{1,0:T(8,128)(2,1)S(1)}, bf16[64,2048]{1,0:T(8,128)(2,1)S(1)}, u32[]{:S(2)}, u32[]{:S(2)}) collective-permute-start(bf16[64,2048]{1,0:T(8,128)(2,1)S(1)} %constant_dynamic-update-slice_fusion.near), channel_id=1, source_target_pairs={{0,1},{1,0},{2,3},{3,2},{4,5},{5,4},{6,7},{7,6},{8,9},{9,8},{10,11... | collective-permute-start | bytes 786440 | tf_op jit(solution)/shard_map/ppermute | solution.py:23
  12.5 1.9 %copy-start.1 = (bf16[2048,768]{1,0:T(8,128)(2,1)S(1)}, bf16[2048,768]{1,0:T(8,128)(2,1)}, u32[]{:S(2)}) copy-start(bf16[2048,768]{1,0:T(8,128)(2,1)} %cold_gate.1) | copy-start | bytes 9437188
  14.4 1.9 %copy-start.2 = (bf16[2048,768]{1,0:T(8,128)(2,1)S(1)}, bf16[2048,768]{1,0:T(8,128)(2,1)}, u32[]{:S(2)}) copy-start(bf16[2048,768]{1,0:T(8,128)(2,1)} %cold_up.1) | copy-start | bytes 9437188
  16.2 1.0 %copy-start.3 = (bf16[2048,128]{1,0:T(8,128)(2,1)S(1)}, bf16[2048,128]{1,0:T(8,128)(2,1)}, u32[]{:S(2)}) copy-start(bf16[2048,128]{1,0:T(8,128)(2,1)} %hot_gate.1) | copy-start | bytes 1572868
  17.3 1.0 %copy-start.4 = (bf16[2048,128]{1,0:T(8,128)(2,1)S(1)}, bf16[2048,128]{1,0:T(8,128)(2,1)}, u32[]{:S(2)}) copy-start(bf16[2048,128]{1,0:T(8,128)(2,1)} %hot_up.1) | copy-start | bytes 1572868
  18.3 23.0 %copy-start = (bf16[768,2048]{1,0:T(8,128)(2,1)S(1)}, bf16[768,2048]{1,0:T(8,128)(2,1)}, u32[]{:S(2)}) copy-start(bf16[768,2048]{1,0:T(8,128)(2,1)} %cold_down.1) | copy-start | bytes 9437188
  18.3 23.0 %copy-start.5 = (bf16[128,2048]{1,0:T(8,128)(2,1)S(1)}, bf16[128,2048]{1,0:T(8,128)(2,1)}, u32[]{:S(2)}) copy-start(bf16[128,2048]{1,0:T(8,128)(2,1)} %hot_down.1) | copy-start | bytes 1572868
  22.9 4.6 %collective-permute-start.4 = (bf16[16,2048]{1,0:T(8,128)(2,1)S(1)}, bf16[16,2048]{1,0:T(8,128)(2,1)S(1)}, u32[]{:S(2)}, u32[]{:S(2)}) collective-permute-start(bf16[16,2048]{1,0:T(8,128)(2,1)S(1)} %get-tuple-element.20), channel_id=1, source_target_pairs={{0,8},{8,0},{16,24},{24,16},{1,9},{9,1},{17,25},{25,17},{2,10},{10... | collective-permute-start | bytes 196616 | tf_op jit(solution)/shard_map/ppermute | solution.py:23
  24.6 7.0 %collective-permute-start.5 = (bf16[16,2048]{1,0:T(8,128)(2,1)S(1)}, bf16[16,2048]{1,0:T(8,128)(2,1)S(1)}, u32[]{:S(2)}, u32[]{:S(2)}) collective-permute-start(bf16[16,2048]{1,0:T(8,128)(2,1)S(1)} %get-tuple-element.21), channel_id=1, source_target_pairs={{0,16},{8,24},{16,0},{24,8},{1,17},{9,25},{17,1},{25,9},{2,18},{10... | collective-permute-start | bytes 196616 | tf_op jit(solution)/shard_map/ppermute | solution.py:23
  27.2 6.1 %collective-permute-start.6 = (bf16[16,2048]{1,0:T(8,128)(2,1)S(1)}, bf16[16,2048]{1,0:T(8,128)(2,1)S(1)}, u32[]{:S(2)}, u32[]{:S(2)}) collective-permute-start(bf16[16,2048]{1,0:T(8,128)(2,1)S(1)} %get-tuple-element.22), channel_id=1, source_target_pairs={{0,24},{8,16},{16,8},{24,0},{1,25},{9,17},{17,9},{25,1},{2,26},{10... | collective-permute-start | bytes 196616 | tf_op jit(solution)/shard_map/ppermute | solution.py:23
  33.9 5.8 %collective-permute-start.9 = (bf16[16,1024]{1,0:T(8,128)(2,1)S(1)}, bf16[16,1024]{1,0:T(8,128)(2,1)S(1)}, u32[]{:S(2)}, u32[]{:S(2)}) collective-permute-start(bf16[16,1024]{1,0:T(8,128)(2,1)S(1)} %act.1.rest_0_), channel_id=1, source_target_pairs={{0,24},{8,16},{16,8},{24,0},{1,25},{9,17},{17,9},{25,1},{2,26},{10... | collective-permute-start | bytes 98312 | tf_op jit(solution)/shard_map/ppermute | solution.py:23
  36.4 5.0 %collective-permute-start.8 = (bf16[16,1024]{1,0:T(8,128)(2,1)S(1)}, bf16[16,1024]{1,0:T(8,128)(2,1)S(1)}, u32[]{:S(2)}, u32[]{:S(2)}) collective-permute-start(bf16[16,1024]{1,0:T(8,128)(2,1)S(1)} %act.1.rest_0_), channel_id=1, source_target_pairs={{0,16},{8,24},{16,0},{24,8},{1,17},{9,25},{17,1},{25,9},{2,18},{10... | collective-permute-start | bytes 98312 | tf_op jit(solution)/shard_map/ppermute | solution.py:23
  36.7 4.7 %collective-permute-start.7 = (bf16[16,1024]{1,0:T(8,128)(2,1)S(1)}, bf16[16,1024]{1,0:T(8,128)(2,1)S(1)}, u32[]{:S(2)}, u32[]{:S(2)}) collective-permute-start(bf16[16,1024]{1,0:T(8,128)(2,1)S(1)} %act.1.rest_0_), channel_id=1, source_target_pairs={{0,8},{8,0},{16,24},{24,16},{1,9},{9,1},{17,25},{25,17},{2,10},{10... | collective-permute-start | bytes 98312 | tf_op jit(solution)/shard_map/ppermute | solution.py:23
  44.9 1.6 %collective-permute-start.10 = (bf16[64,2048]{1,0:T(8,128)(2,1)S(1)}, bf16[64,2048]{1,0:T(8,128)(2,1)S(1)}, u32[]{:S(2)}, u32[]{:S(2)}) collective-permute-start(bf16[64,2048]{1,0:T(8,128)(2,1)S(1)} %get-tuple-element.24), channel_id=1, source_target_pairs={{0,1},{1,0},{2,3},{3,2},{4,5},{5,4},{6,7},{7,6},{8,9},{9,8},{10,11... | collective-permute-start | bytes 786440 | tf_op jit(solution)/shard_map/ppermute | solution.py:23
  46.6 4.9 %collective-permute-start.11 = (bf16[16,2048]{1,0:T(8,128)(2,1)S(1)}, bf16[16,2048]{1,0:T(8,128)(2,1)S(1)}, u32[]{:S(2)}, u32[]{:S(2)}) collective-permute-start(bf16[16,2048]{1,0:T(8,128)(2,1)S(1)} %get-tuple-element.27), channel_id=1, source_target_pairs={{0,2},{1,3},{2,0},{3,1},{4,6},{5,7},{6,4},{7,5},{8,10},{9,11},{10,... | collective-permute-start | bytes 196616 | tf_op jit(solution)/shard_map/ppermute | solution.py:23
  47.2 5.2 %collective-permute-start.13 = (bf16[16,2048]{1,0:T(8,128)(2,1)S(1)}, bf16[16,2048]{1,0:T(8,128)(2,1)S(1)}, u32[]{:S(2)}, u32[]{:S(2)}) collective-permute-start(bf16[16,2048]{1,0:T(8,128)(2,1)S(1)} %get-tuple-element.28), channel_id=1, source_target_pairs={{0,6},{1,7},{2,4},{3,5},{4,2},{5,3},{6,0},{7,1},{8,14},{9,15},{10,... | collective-permute-start | bytes 196616 | tf_op jit(solution)/shard_map/ppermute | solution.py:23
  48.7 4.8 %collective-permute-start.12 = (bf16[16,2048]{1,0:T(8,128)(2,1)S(1)}, bf16[16,2048]{1,0:T(8,128)(2,1)S(1)}, u32[]{:S(2)}, u32[]{:S(2)}) collective-permute-start(bf16[16,2048]{1,0:T(8,128)(2,1)S(1)} %get-tuple-element.29), channel_id=1, source_target_pairs={{0,4},{1,5},{2,6},{3,7},{4,0},{5,1},{6,2},{7,3},{8,12},{9,13},{10,... | collective-permute-start | bytes 196616 | tf_op jit(solution)/shard_map/ppermute | solution.py:23

commit v2 on v1

v2 whole, which is shorter than its diff:
```python
import functools

import jax
import jax.numpy as jnp
from jax import lax
from jax.experimental import pallas as pl
from jax.experimental.pallas import tpu as pltpu
from jax.sharding import PartitionSpec as P

BLOCK = 128
F32 = jnp.float32
BF16 = jnp.bfloat16
WIRE = jnp.bfloat16
VM = pl.BlockSpec(memory_space=pltpu.VMEM)
SM = pl.BlockSpec(memory_space=pltpu.SMEM)
HB = pl.BlockSpec(memory_space=pltpu.HBM)


def cost(flops):
    return pl.CostEstimate(flops=flops, bytes_accessed=0, transcendentals=0)


def params(mib):
    return pltpu.CompilerParams(vmem_limit_bytes=mib * 1024 * 1024)


def send(value, axis, size, mask):
    return lax.ppermute(value, axis, [(at, at ^ mask) for at in range(size)])


def route_kernel(
    cold_at, cold_ids, hot_ids, mask, *rest, order, rows, cold_blocks, hot_blocks, weights
):
    sources = rest[:weights]
    pick, spread, row_bits, bits = rest[weights : weights + 4]
    targets = rest[weights + 4 : 2 * weights + 4]
    ordered, sems = rest[2 * weights + 4 :]
    copies = [
        pltpu.make_async_copy(a, b, sems.at[n]) for n, (a, b) in enumerate(zip(sources, targets))
    ]
    for copy in copies:
        copy.start()
    total, named = mask.shape
    own = cold_at[0]
    for at, mark in enumerate(order):
        first = pl.multiple_of((own ^ mark) * rows, rows)
        ordered[at * rows : (at + 1) * rows, :] = mask[pl.ds(first, rows), :]
    width = bits.shape[1]
    wanted = jnp.full((width, named), -1, jnp.int32)
    row = lax.broadcasted_iota(jnp.int32, (width, named), 0)
    for at in range(cold_blocks):
        wanted = jnp.where(row == at, cold_ids[own * cold_blocks + at], wanted)
    for at in range(hot_blocks):
        wanted = jnp.where(row == cold_blocks + at, hot_ids[own * hot_blocks + at], wanted)
    column = lax.broadcasted_iota(jnp.int32, (width, named), 1)
    choose = (wanted == column).astype(F32).astype(BF16)
    active = ordered[...].astype(F32).astype(BF16)
    contract = (((1,), (1,)), ((), ()))
    by_token = lax.dot_general(active, choose, contract, preferred_element_type=F32)
    by_block = lax.dot_general(choose, active, contract, preferred_element_type=F32)
    bits[...] = by_token
    lane = lax.broadcasted_iota(jnp.int32, by_token.shape, 1)
    hit_col = jnp.max(jnp.where(lane < cold_blocks, by_token, 0.0), axis=1, keepdims=True)
    line = lax.broadcasted_iota(jnp.int32, by_block.shape, 0)
    hit_row = jnp.max(jnp.where(line < cold_blocks, by_block, 0.0), axis=0, keepdims=True)
    down = lax.broadcasted_iota(jnp.int32, (total, total), 0)
    across = lax.broadcasted_iota(jnp.int32, (total, total), 1)
    rank_col = jnp.sum(jnp.where(across < down, hit_row, 0.0), axis=1, keepdims=True)
    rank_row = jnp.sum(jnp.where(down < across, hit_col, 0.0), axis=0, keepdims=True)
    slot_row = jnp.where(hit_row > 0.0, rank_row, -1.0)
    slot_col = jnp.where(hit_col > 0.0, rank_col, -1.0)
    slots = total // 2
    chosen = lax.broadcasted_iota(jnp.int32, (slots, total), 0).astype(F32) == slot_row
    chosen = chosen.astype(F32).astype(BF16)
    pick[...] = chosen
    back = lax.broadcasted_iota(jnp.int32, (total, slots), 1).astype(F32) == slot_col
    spread[...] = back.astype(F32).astype(BF16)
    row_bits[...] = jnp.dot(chosen, by_token.astype(BF16), preferred_element_type=F32)
    for copy in copies:
        copy.wait()


def chunk_of(width):
    return 256 if width % 256 == 0 else 128


def up_kernel(hot_at, near, far, pick, hot_gate, hot_up, cold_gate, cold_up, *rest, parts):
    outs = rest[:parts]
    sums = rest[parts]
    cold_width = cold_gate.shape[1]
    hot_width = hot_gate.shape[1]
    step = chunk_of(cold_width)
    half = near.shape[0]
    gates = cold_width + 2 * hot_width
    near_rows = near[...]
    far_rows = far[...]
    picked = jnp.dot(pick[:, :half], near_rows, preferred_element_type=F32)
    picked = picked + jnp.dot(pick[:, half:], far_rows, preferred_element_type=F32)
    picked = picked.astype(BF16)
    for base, weight in ((0, hot_gate), (gates, hot_up)):
        for side, rows in enumerate((near_rows, far_rows)):
            at = base + cold_width + side * hot_width
            sums[:, at : at + hot_width] = jnp.dot(rows, weight[...], preferred_element_type=F32)
    for base, weight in ((0, cold_gate), (gates, cold_up)):
        for at in range(0, cold_width, step):
            value = jnp.dot(picked, weight[:, at : at + step], preferred_element_type=F32)
            sums[:, base + at : base + at + step] = value
    share = half // parts
    for mark, out in enumerate(outs):
        first = pl.multiple_of((hot_at[0] ^ mark) * share, share)
        out[...] = sums[pl.ds(first, share), :].astype(out.dtype)


def act_kernel(hot_at, row_bits, bits, *rest, cold_blocks, hot_blocks):
    out = rest[-1]
    terms = rest[:-1]
    share = out.shape[0]
    gates = out.shape[1]
    slots = row_bits.shape[0]
    total = terms[0][...].astype(F32)
    for term in terms[1:]:
        total = total + term[...].astype(F32)
    first = pl.multiple_of(hot_at[0] * share, share)
    cold_rows = row_bits[pl.ds(first, share), :]
    columns = [cold_rows[:, at : at + 1] for at in range(cold_blocks)]
    for side in range(2):
        begin = pl.multiple_of(side * slots + hot_at[0] * share, share)
        hot_rows = bits[pl.ds(begin, share), :]
        columns += [hot_rows[:, cold_blocks + at : cold_blocks + at + 1] for at in range(hot_blocks)]
    for at, column in enumerate(columns):
        gate = total[:, at * BLOCK : (at + 1) * BLOCK]
        up = total[:, gates + at * BLOCK : gates + (at + 1) * BLOCK]
        value = gate / (1.0 + jnp.exp(-gate)) * up * column
        out[:, at * BLOCK : (at + 1) * BLOCK] = value.astype(BF16)


def down_kernel(hot_at, spread, cold_down, hot_down, *rest, parts, side):
    blocks = rest[:parts]
    out, hidden = rest[parts:]
    cold_width, features = cold_down.shape
    hot_width = hot_down.shape[0]
    step = chunk_of(features)
    share = blocks[0].shape[0]
    for mark, block in enumerate(blocks):
        first = pl.multiple_of((hot_at[0] ^ mark) * share, share)
        hidden[pl.ds(first, share), :] = block[...]
    half = out.shape[0]
    rows = spread[side * half : (side + 1) * half, :]
    cold_rows = jnp.dot(rows, hidden[:, :cold_width], preferred_element_type=F32).astype(BF16)
    first = cold_width + side * hot_width
    hot_rows = hidden[:, first : first + hot_width]
    for at in range(0, features, step):
        value = jnp.dot(cold_rows, cold_down[:, at : at + step], preferred_element_type=F32)
        value = value + jnp.dot(hot_rows, hot_down[:, at : at + step], preferred_element_type=F32)
        out[:, at : at + step] = value.astype(out.dtype)


def body(
    tokens, hot_gate, hot_up, hot_down, cold_gate, cold_up, cold_down, hot_ids, cold_ids, block_mask
):
    groups = lax.axis_size("cold")
    ranges = lax.axis_size("hot")
    cold_at = lax.axis_index("cold").astype(jnp.int32).reshape(1)
    hot_at = lax.axis_index("hot").astype(jnp.int32).reshape(1)
    rows, features = tokens.shape
    total, named = block_mask.shape
    half = total // 2
    share = half // ranges
    hot_width = hot_gate.shape[1]
    cold_width = cold_gate.shape[1]
    hot_blocks = hot_width // BLOCK
    cold_blocks = cold_width // BLOCK
    gates = cold_width + 2 * hot_width
    order = list(range(0, groups, 2)) + list(range(1, groups, 2))
    bits_width = -(-(cold_blocks + hot_blocks) // 8) * 8

    near = [tokens] + [send(tokens, "cold", groups, mark) for mark in range(2, groups, 2)]
    near = jnp.concatenate(near, axis=0)
    far = send(near, "cold", groups, 1)

    weights = (hot_gate, hot_up, cold_gate, cold_up)
    weights = tuple(pltpu.with_memory_space_constraint(item, pltpu.HBM) for item in weights)
    routed = pl.pallas_call(
        functools.partial(
            route_kernel,
            order=order,
            rows=rows,
            cold_blocks=cold_blocks,
            hot_blocks=hot_blocks,
            weights=len(weights),
        ),
        out_shape=(
            jax.ShapeDtypeStruct((half, total), BF16),
            jax.ShapeDtypeStruct((total, half), BF16),
            jax.ShapeDtypeStruct((half, bits_width), F32),
            jax.ShapeDtypeStruct((total, bits_width), F32),
            *(jax.ShapeDtypeStruct(weight.shape, weight.dtype) for weight in weights),
        ),
        in_specs=[SM, SM, SM, VM] + [HB] * len(weights),
        out_specs=(VM,) * (4 + len(weights)),
        scratch_shapes=[
            pltpu.VMEM((total, named), jnp.int32),
            pltpu.SemaphoreType.DMA((len(weights),)),
        ],
        compiler_params=params(24),
        cost_estimate=cost(50_000_000),
        name="route",
    )(cold_at, cold_ids, hot_ids, block_mask, *weights)
    pick, spread, row_bits, bits = routed[:4]

    partial_sums = pl.pallas_call(
        functools.partial(up_kernel, parts=ranges),
        out_shape=tuple(
            jax.ShapeDtypeStruct((share, 2 * gates), WIRE if mark else F32) for mark in range(ranges)
        ),
        in_specs=[SM, VM, VM, VM, VM, VM, VM, VM],
        out_specs=tuple(VM for _ in range(ranges)),
        scratch_shapes=[pltpu.VMEM((half, 2 * gates), F32)],
        compiler_params=params(24),
        name="up",
    )(hot_at, near, far, pick, *routed[4:])

    terms = [partial_sums[0]]
    terms += [send(partial_sums[mark], "hot", ranges, mark) for mark in range(1, ranges)]
    own_hidden = pl.pallas_call(
        functools.partial(act_kernel, cold_blocks=cold_blocks, hot_blocks=hot_blocks),
        out_shape=jax.ShapeDtypeStruct((share, gates), BF16),
        in_specs=[SM, VM, VM] + [VM] * ranges,
        out_specs=VM,
        compiler_params=params(16),
        name="act",
    )(hot_at, row_bits, bits, *terms)

    blocks = [own_hidden] + [send(own_hidden, "hot", ranges, mark) for mark in range(1, ranges)]

    def down(side, kind):
        return pl.pallas_call(
            functools.partial(down_kernel, parts=ranges, side=side),
            out_shape=jax.ShapeDtypeStruct((half, features), kind),
            in_specs=[SM, VM, VM, VM] + [VM] * ranges,
            out_specs=VM,
            scratch_shapes=[pltpu.VMEM((half, gates), BF16)],
            compiler_params=params(24),
            cost_estimate=cost(20_000_000),
            name=f"down{side}",
        )(hot_at, spread, cold_down, hot_down, *blocks)

    far_back = send(down(1, BF16), "cold", groups, 1)
    pair = down(0, F32) + far_back.astype(F32)
    result = pair[:rows]
    for at in range(1, groups // 2):
        piece = pair[at * rows : (at + 1) * rows].astype(BF16)
        result = result + send(piece, "cold", groups, 2 * at).astype(F32)
    return result.astype(BF16)


def solution(mesh):
    return jax.shard_map(
        body,
        mesh=mesh,
        in_specs=(
            P("cold", "hot"),
            P("hot", "cold"),
            P("hot", "cold"),
            P("cold", "hot"),
            P("hot", "cold"),
            P("hot", "cold"),
            P("cold", "hot"),
            P(),
            P(),
            P(),
        ),
        out_specs=P("cold", "hot"),
        check_vma=False,
    )
```

time: 54.6 us -> 46.8 us (0.86)
  local copies, waits for them, and re-layouts: 7.65 us -> 3.1 us
  Pallas kernels: 9.69 us -> 7.49 us
  other arithmetic: 1.55 us -> 0.73 us
    unnamed x16 -> x12, local copies, waits for them, and re-layouts: 7.63 us -> 3.08 us
    pallas_call x1, Pallas kernels: 0.9 us -> 3.92 us  [body(): pl.pallas_call(functools.partial(route_kernel, order=order, rows=rows, co...]
    pallas_call x1, Pallas kernels: 4.59 us -> 1.76 us  [body(): pl.pallas_call(functools.partial(up_kernel, parts=ranges), out_shape=tupl...]
    pallas_call x1 -> x2, Pallas kernels: 3.57 us -> 1.7 us  [down(): pl.pallas_call(functools.partial(down_kernel, parts=ranges, side=side), o...]
    concatenate x1 -> x0, other arithmetic: 0.75 us -> none  [body(): ids = jnp.concatenate([cold_ids, hot_ids])]
  transfers between devices with their start and end apart: 14 -> 14, of which waited for: 11 -> 11; matrix products, arithmetic and copies ran while one was open for 5% -> 4% of each run, Pallas kernels for 2% -> 10%
where the time goes in v2:
time: 46.8 us; the launch traced here: 46.5 us
  waiting for transfers between devices  18.1 us (39%)
  starting transfers between devices  17 us (36%)
  Pallas kernels  7.49 us (16%)
  local copies, waits for them, and re-layouts  3.1 us (7%)
  other arithmetic  0.73 us (2%)
    ppermute x14, waiting for transfers between devices, send(): return lax.ppermute(value, axis, [(at, at ^ mask) for at in range(size)])  18.1 us
    ppermute x14, starting transfers between devices, send(): return lax.ppermute(value, axis, [(at, at ^ mask) for at in range(size)])  17 us
    pallas_call x1, Pallas kernels, body(): pl.pallas_call(functools.partial(route_kernel, order=order, rows=rows, co...  3.92 us
    unnamed x12, local copies, waits for them, and re-layouts  3.08 us
    pallas_call x1, Pallas kernels, body(): pl.pallas_call(functools.partial(up_kernel, parts=ranges), out_shape=tupl...  1.76 us
    pallas_call x2, Pallas kernels, down(): pl.pallas_call(functools.partial(down_kernel, parts=ranges, side=side), o...  1.7 us
  transfers between devices with their start and end apart: 14, of which 11 were waited for; matrix products, arithmetic and copies ran while one was open for 4% of the time, Pallas kernels for 10%

profile of v2, /device:TPU:0, one launch (start us, length us, event | category | flops | bytes accessed | tf_op | source)
XLA Modules:
  0.0 46.5 jit_solution(11887275110956508672)
XLA Ops:
  0.0 3.0 %collective-permute-start = (bf16[16,2048]{1,0:T(8,128)(2,1)}, bf16[16,2048]{1,0:T(8,128)(2,1)S(1)}, u32[]{:S(2)}, u32[]{:S(2)}) collective-permute-start(bf16[16,2048]{1,0:T(8,128)(2,1)} %param.10), channel_id=1, source_target_pairs={{0,2},{1,3},{2,0},{3,1},{4,6},{5,7},{6,4},{7,5},{8,10},{9,11},{10,... | collective-permute-start | bytes 196616 | tf_op jit(solution)/shard_map/ppermute | solution.py:28
  3.0 1.5 %collective-permute-start.1 = (bf16[16,2048]{1,0:T(8,128)(2,1)}, bf16[16,2048]{1,0:T(8,128)(2,1)S(1)}, u32[]{:S(2)}, u32[]{:S(2)}) collective-permute-start(bf16[16,2048]{1,0:T(8,128)(2,1)} %param.10), channel_id=1, source_target_pairs={{0,4},{1,5},{2,6},{3,7},{4,0},{5,1},{6,2},{7,3},{8,12},{9,13},{10,... | collective-permute-start | bytes 196616 | tf_op jit(solution)/shard_map/ppermute | solution.py:28
  4.5 0.0 collective-permute-start.2
  4.5 0.9 %constant_dynamic-update-slice_fusion.3 = bf16[64,2048]{1,0:T(8,128)(2,1)S(1)} fusion(bf16[16,2048]{1,0:T(8,128)(2,1)} %param.10), kind=kLoop, calls=%fused_computation.8 | loop fusion | bytes 131072
  5.4 0.2 collective-permute-done
  5.6 1.8 %collective-permute-done.1 = bf16[16,2048]{1,0:T(8,128)(2,1)S(1)} collective-permute-done((bf16[16,2048]{1,0:T(8,128)(2,1)}, bf16[16,2048]{1,0:T(8,128)(2,1)S(1)}, u32[]{:S(2)}, u32[]{:S(2)}) %collective-permute-start.1) | collective-permute-done | bytes 65568 | tf_op jit(solution)/shard_map/ppermute | solution.py:28
  7.5 2.4 %collective-permute-done.2 = bf16[16,2048]{1,0:T(8,128)(2,1)S(1)} collective-permute-done((bf16[16,2048]{1,0:T(8,128)(2,1)}, bf16[16,2048]{1,0:T(8,128)(2,1)S(1)}, u32[]{:S(2)}, u32[]{:S(2)}) %collective-permute-start.2) | collective-permute-done | bytes 65568 | tf_op jit(solution)/shard_map/ppermute | solution.py:28
  9.9 0.0 collective-permute-start.3
  9.9 0.8 %copy.11.mask = s32[128,56]{1,0:T(8,128)S(1)} copy(s32[128,56]{0,1:T(8,128)} %param.19) | data formatting | bytes 57344 | tf_op args[9]
  10.7 0.0 copy-start.2
  10.7 0.6 %copy-done.2 = s32[48]{0:T(128)S(1)} copy-done((s32[48]{0:T(128)S(1)}, s32[48]{0:T(128)}, u32[]{:S(2)}) %copy-start.2) | copy-done | bytes 216
  11.4 0.0 copy-start.3
  11.4 0.7 %copy-done.3 = s32[8]{0:T(128)S(1)} copy-done((s32[8]{0:T(128)S(1)}, s32[8]{0:T(128)}, u32[]{:S(2)}) %copy-start.3) | copy-done | bytes 56
  12.0 3.9 %route.1 = (bf16[64,128]{1,0:T(8,128)(2,1)S(1)}, bf16[128,64]{1,0:T(8,128)(2,1)S(1)}, f32[64,8]{1,0:T(8,128)S(1)}, f32[128,8]{1,0:T(8,128)S(1)}, bf16[2048,128]{...) custom-call(s32[1]{0:T(128)} %bitcast.1.cold_at, ...), custom_call_target="tpu_custom_call" | custom-call | flops 50000000 | tf_op jit(solution)/shard_map/route/pallas_call | solution.py:183
  16.0 0.0 collective-permute-done.3.far
  16.0 0.0 copy-start
  16.0 0.0 copy-start.1
  16.0 1.8 %up.1 = (f32[16,2048]{1,0:T(8,128)S(1)}, bf16[16,2048]{1,0:T(8,128)(2,1)S(1)}, bf16[16,2048]{1,0:T(8,128)(2,1)S(1)}, bf16[16,2048]{1,0:T(8,128)(2,1)S(1)}) custom-call(s32[1]{0:T(128)} %bitcast.hot_at, bf16[64,2048]{1,0:T(8,128)(2,1)S(1)} %constant_dynamic-update-slice_fusion.near, bf16[64,2048]{1,0:T(8,128)(2,1)S(1)} %collective-permute-done.3.far, ...), custom_call_target="tpu_custom_call" | custom-call | tf_op jit(solution)/shard_map/up/pallas_call | solution.py:211
  17.8 1.6 %collective-permute-start.4 = (bf16[16,2048]{1,0:T(8,128)(2,1)S(1)}, bf16[16,2048]{1,0:T(8,128)(2,1)S(1)}, u32[]{:S(2)}, u32[]{:S(2)}) collective-permute-start(bf16[16,2048]{1,0:T(8,128)(2,1)S(1)} %get-tuple-element.26), channel_id=1, source_target_pairs={{0,8},{8,0},{16,24},{24,16},{1,9},{9,1},{17,25},{25,17},{2,10},{10... | collective-permute-start | bytes 196616 | tf_op jit(solution)/shard_map/ppermute | solution.py:28
  19.4 2.6 %collective-permute-start.5 = (bf16[16,2048]{1,0:T(8,128)(2,1)S(1)}, bf16[16,2048]{1,0:T(8,128)(2,1)S(1)}, u32[]{:S(2)}, u32[]{:S(2)}) collective-permute-start(bf16[16,2048]{1,0:T(8,128)(2,1)S(1)} %get-tuple-element.27), channel_id=1, source_target_pairs={{0,16},{8,24},{16,0},{24,8},{1,17},{9,25},{17,1},{25,9},{2,18},{10... | collective-permute-start | bytes 196616 | tf_op jit(solution)/shard_map/ppermute | solution.py:28
  22.0 0.2 collective-permute-start.6
  22.2 0.1 collective-permute-done.4.rest_1_
  22.4 4.1 %collective-permute-done.5.rest_2_ = bf16[16,2048]{1,0:T(8,128)(2,1)S(1)} collective-permute-done((bf16[16,2048]{1,0:T(8,128)(2,1)S(1)}, bf16[16,2048]{1,0:T(8,128)(2,1)S(1)}, u32[]{:S(2)}, u32[]{:S(2)}) %collective-permute-start.5) | collective-permute-done | bytes 65568 | tf_op jit(solution)/shard_map/ppermute | solution.py:28
  26.4 1.7 %collective-permute-done.6.rest_3_ = bf16[16,2048]{1,0:T(8,128)(2,1)S(1)} collective-permute-done((bf16[16,2048]{1,0:T(8,128)(2,1)S(1)}, bf16[16,2048]{1,0:T(8,128)(2,1)S(1)}, u32[]{:S(2)}, u32[]{:S(2)}) %collective-permute-start.6) | collective-permute-done | bytes 65568 | tf_op jit(solution)/shard_map/ppermute | solution.py:28
  28.1 0.1 act.1.rest_0_
  28.2 1.3 %collective-permute-start.7 = (bf16[16,1024]{1,0:T(8,128)(2,1)S(1)}, bf16[16,1024]{1,0:T(8,128)(2,1)S(1)}, u32[]{:S(2)}, u32[]{:S(2)}) collective-permute-start(bf16[16,1024]{1,0:T(8,128)(2,1)S(1)} %act.1.rest_0_), channel_id=1, source_target_pairs={{0,8},{8,0},{16,24},{24,16},{1,9},{9,1},{17,25},{25,17},{2,10},{10... | collective-permute-start | bytes 98312 | tf_op jit(solution)/shard_map/ppermute | solution.py:28
  29.5 1.7 %collective-permute-start.8 = (bf16[16,1024]{1,0:T(8,128)(2,1)S(1)}, bf16[16,1024]{1,0:T(8,128)(2,1)S(1)}, u32[]{:S(2)}, u32[]{:S(2)}) collective-permute-start(bf16[16,1024]{1,0:T(8,128)(2,1)S(1)} %act.1.rest_0_), channel_id=1, source_target_pairs={{0,16},{8,24},{16,0},{24,8},{1,17},{9,25},{17,1},{25,9},{2,18},{10... | collective-permute-start | bytes 98312 | tf_op jit(solution)/shard_map/ppermute | solution.py:28
  31.3 1.4 %collective-permute-start.9 = (bf16[16,1024]{1,0:T(8,128)(2,1)S(1)}, bf16[16,1024]{1,0:T(8,128)(2,1)S(1)}, u32[]{:S(2)}, u32[]{:S(2)}) collective-permute-start(bf16[16,1024]{1,0:T(8,128)(2,1)S(1)} %act.1.rest_0_), channel_id=1, source_target_pairs={{0,24},{8,16},{16,8},{24,0},{1,25},{9,17},{17,9},{25,1},{2,26},{10... | collective-permute-start | bytes 98312 | tf_op jit(solution)/shard_map/ppermute | solution.py:28
  32.6 0.0 collective-permute-done.7.rest_1_
  32.6 2.3 %collective-permute-done.8.rest_2_ = bf16[16,1024]{1,0:T(8,128)(2,1)S(1)} collective-permute-done((bf16[16,1024]{1,0:T(8,128)(2,1)S(1)}, bf16[16,1024]{1,0:T(8,128)(2,1)S(1)}, u32[]{:S(2)}, u32[]{:S(2)}) %collective-permute-start.8) | collective-permute-done | bytes 32800 | tf_op jit(solution)/shard_map/ppermute | solution.py:28
  34.9 2.1 %collective-permute-done.9.rest_3_ = bf16[16,1024]{1,0:T(8,128)(2,1)S(1)} collective-permute-done((bf16[16,1024]{1,0:T(8,128)(2,1)S(1)}, bf16[16,1024]{1,0:T(8,128)(2,1)S(1)}, u32[]{:S(2)}, u32[]{:S(2)}) %collective-permute-start.9) | collective-permute-done | bytes 32800 | tf_op jit(solution)/shard_map/ppermute | solution.py:28
  37.0 0.0 copy-done
  37.0 0.0 copy-done.1
  37.0 0.8 %down1.1 = bf16[64,2048]{1,0:T(8,128)(2,1)S(1)} custom-call(s32[1]{0:T(128)} %bitcast.hot_at, bf16[128,64]{1,0:T(8,128)(2,1)S(1)} %get-tuple-element.17.spread, bf16[768,2048]{1,0:T(8,128)(2,1)S(1)} %copy-done, bf16[128,2048]{1,0:T(8,128)(2,1)S(1)} %copy-done.1, bf16[16,1024]{1,0:T(8,128)(2,1)S(1)} %act.1.rest_0_, ...), custom_call_target="tpu_custom_call" | custom-call | flops 20000000 | tf_op jit(solution)/shard_map/down1/pallas_call | solution.py:237
  37.8 0.1 collective-permute-start.10
  37.9 0.9 %down0.1 = f32[64,2048]{1,0:T(8,128)S(1)} custom-call(s32[1]{0:T(128)} %bitcast.hot_at, bf16[128,64]{1,0:T(8,128)(2,1)S(1)} %get-tuple-element.17.spread, bf16[768,2048]{1,0:T(8,128)(2,1)S(1)} %copy-done, bf16[128,2048]{1,0:T(8,128)(2,1)S(1)} %copy-done.1, bf16[16,1024]{1,0:T(8,128)(2,1)S(1)} %act.1.rest_0_, ...), custom_call_target="tpu_custom_call" | custom-call | flops 20000000 | tf_op jit(solution)/shard_map/down0/pallas_call | solution.py:237
  38.8 0.7 %collective-permute-done.10 = bf16[64,2048]{1,0:T(8,128)(2,1)S(1)} collective-permute-done((bf16[64,2048]{1,0:T(8,128)(2,1)S(1)}, bf16[64,2048]{1,0:T(8,128)(2,1)S(1)}, u32[]{:S(2)}, u32[]{:S(2)}) %collective-permute-start.10) | collective-permute-done | bytes 262176 | tf_op jit(solution)/shard_map/ppermute | solution.py:28
  39.4 0.1 fusion.3
  39.5 0.5 %collective-permute-start.13 = (bf16[16,2048]{1,0:T(8,128)(2,1)S(1)}, bf16[16,2048]{1,0:T(8,128)(2,1)S(1)}, u32[]{:S(2)}, u32[]{:S(2)}) collective-permute-start(bf16[16,2048]{1,0:T(8,128)(2,1)S(1)} %get-tuple-element.32), channel_id=1, source_target_pairs={{0,6},{1,7},{2,4},{3,5},{4,2},{5,3},{6,0},{7,1},{8,14},{9,15},{10,... | collective-permute-start | bytes 196616 | tf_op jit(solution)/shard_map/ppermute | solution.py:28
  40.1 1.5 %collective-permute-start.12 = (bf16[16,2048]{1,0:T(8,128)(2,1)S(1)}, bf16[16,2048]{1,0:T(8,128)(2,1)S(1)}, u32[]{:S(2)}, u32[]{:S(2)}) collective-permute-start(bf16[16,2048]{1,0:T(8,128)(2,1)S(1)} %get-tuple-element.33), channel_id=1, source_target_pairs={{0,4},{1,5},{2,6},{3,7},{4,0},{5,1},{6,2},{7,3},{8,12},{9,13},{10,... | collective-permute-start | bytes 196616 | tf_op jit(solution)/shard_map/ppermute | solution.py:28
  41.6 1.5 %collective-permute-start.11 = (bf16[16,2048]{1,0:T(8,128)(2,1)S(1)}, bf16[16,2048]{1,0:T(8,128)(2,1)S(1)}, u32[]{:S(2)}, u32[]{:S(2)}) collective-permute-start(bf16[16,2048]{1,0:T(8,128)(2,1)S(1)} %get-tuple-element.31), channel_id=1, source_target_pairs={{0,2},{1,3},{2,0},{3,1},{4,6},{5,7},{6,4},{7,5},{8,10},{9,11},{10,... | collective-permute-start | bytes 196616 | tf_op jit(solution)/shard_map/ppermute | solution.py:28
  43.1 2.2 %collective-permute-done.13 = bf16[16,2048]{1,0:T(8,128)(2,1)S(1)} collective-permute-done((bf16[16,2048]{1,0:T(8,128)(2,1)S(1)}, bf16[16,2048]{1,0:T(8,128)(2,1)S(1)}, u32[]{:S(2)}, u32[]{:S(2)}) %collective-permute-start.13) | collective-permute-done | bytes 65568 | tf_op jit(solution)/shard_map/ppermute | solution.py:28
  45.3 0.0 collective-permute-done.12
  45.3 0.5 %collective-permute-done.11 = bf16[16,2048]{1,0:T(8,128)(2,1)S(1)} collective-permute-done((bf16[16,2048]{1,0:T(8,128)(2,1)S(1)}, bf16[16,2048]{1,0:T(8,128)(2,1)S(1)}, u32[]{:S(2)}, u32[]{:S(2)}) %collective-permute-start.11) | collective-permute-done | bytes 65568 | tf_op jit(solution)/shard_map/ppermute | solution.py:28
  45.9 0.7 %fusion.2 = bf16[16,2048]{1,0:T(8,128)(2,1)} fusion(f32[64,2048]{1,0:T(8,128)S(1)} %get-tuple-element.30, bf16[16,2048]{1,0:T(8,128)(2,1)S(1)} %collective-permute-done.13, bf16[16,2048]{1,0:T(8,128)(2,1)S(1)} %collective-permute-done.12, bf16[16,2048]{1,0:T(8,128)(2,1)S(1)} %collective-permute-done.11), kind=kLoop, calls=%fused_computation.4 | loop fusion | flops 229376 | bytes 393216 | tf_op jit(solution)/shard_map/convert_element_type | solution.py:254
  (4 shorter events, 0.0 us)
Async XLA Ops:
  0.0 5.6 %collective-permute-start = (bf16[16,2048]{1,0:T(8,128)(2,1)}, bf16[16,2048]{1,0:T(8,128)(2,1)S(1)}, u32[]{:S(2)}, u32[]{:S(2)}) collective-permute-start(bf16[16,2048]{1,0:T(8,128)(2,1)} %param.10), channel_id=1, source_target_pairs={{0,2},{1,3},{2,0},{3,1},{4,6},{5,7},{6,4},{7,5},{8,10},{9,11},{10,... | collective-permute-start | bytes 196616 | tf_op jit(solution)/shard_map/ppermute | solution.py:28
  3.0 4.5 %collective-permute-start.1 = (bf16[16,2048]{1,0:T(8,128)(2,1)}, bf16[16,2048]{1,0:T(8,128)(2,1)S(1)}, u32[]{:S(2)}, u32[]{:S(2)}) collective-permute-start(bf16[16,2048]{1,0:T(8,128)(2,1)} %param.10), channel_id=1, source_target_pairs={{0,4},{1,5},{2,6},{3,7},{4,0},{5,1},{6,2},{7,3},{8,12},{9,13},{10,... | collective-permute-start | bytes 196616 | tf_op jit(solution)/shard_map/ppermute | solution.py:28
  4.5 5.4 %collective-permute-start.2 = (bf16[16,2048]{1,0:T(8,128)(2,1)}, bf16[16,2048]{1,0:T(8,128)(2,1)S(1)}, u32[]{:S(2)}, u32[]{:S(2)}) collective-permute-start(bf16[16,2048]{1,0:T(8,128)(2,1)} %param.10), channel_id=1, source_target_pairs={{0,6},{1,7},{2,4},{3,5},{4,2},{5,3},{6,0},{7,1},{8,14},{9,15},{10,... | collective-permute-start | bytes 196616 | tf_op jit(solution)/shard_map/ppermute | solution.py:28
  9.9 6.1 %collective-permute-start.3 = (bf16[64,2048]{1,0:T(8,128)(2,1)S(1)}, bf16[64,2048]{1,0:T(8,128)(2,1)S(1)}, u32[]{:S(2)}, u32[]{:S(2)}) collective-permute-start(bf16[64,2048]{1,0:T(8,128)(2,1)S(1)} %constant_dynamic-update-slice_fusion.near), channel_id=1, source_target_pairs={{0,1},{1,0},{2,3},{3,2},{4,5},{5,4},{6,7},{7,6},{8,9},{9,8},{10,11... | collective-permute-start | bytes 786440 | tf_op jit(solution)/shard_map/ppermute | solution.py:28
  10.7 0.7 %copy-start.2 = (s32[48]{0:T(128)S(1)}, s32[48]{0:T(128)}, u32[]{:S(2)}) copy-start(s32[48]{0:T(128)} %cold_ids.1) | copy-start | bytes 580
  11.4 0.7 %copy-start.3 = (s32[8]{0:T(128)S(1)}, s32[8]{0:T(128)}, u32[]{:S(2)}) copy-start(s32[8]{0:T(128)} %hot_ids.1) | copy-start | bytes 100
  16.0 21.0 %copy-start = (bf16[768,2048]{1,0:T(8,128)(2,1)S(1)}, bf16[768,2048]{1,0:T(8,128)(2,1)}, u32[]{:S(2)}) copy-start(bf16[768,2048]{1,0:T(8,128)(2,1)} %cold_down.3) | copy-start | bytes 9437188
  16.0 21.0 %copy-start.1 = (bf16[128,2048]{1,0:T(8,128)(2,1)S(1)}, bf16[128,2048]{1,0:T(8,128)(2,1)}, u32[]{:S(2)}) copy-start(bf16[128,2048]{1,0:T(8,128)(2,1)} %hot_down.3) | copy-start | bytes 1572868
  17.8 4.6 %collective-permute-start.4 = (bf16[16,2048]{1,0:T(8,128)(2,1)S(1)}, bf16[16,2048]{1,0:T(8,128)(2,1)S(1)}, u32[]{:S(2)}, u32[]{:S(2)}) collective-permute-start(bf16[16,2048]{1,0:T(8,128)(2,1)S(1)} %get-tuple-element.26), channel_id=1, source_target_pairs={{0,8},{8,0},{16,24},{24,16},{1,9},{9,1},{17,25},{25,17},{2,10},{10... | collective-permute-start | bytes 196616 | tf_op jit(solution)/shard_map/ppermute | solution.py:28
  19.4 7.0 %collective-permute-start.5 = (bf16[16,2048]{1,0:T(8,128)(2,1)S(1)}, bf16[16,2048]{1,0:T(8,128)(2,1)S(1)}, u32[]{:S(2)}, u32[]{:S(2)}) collective-permute-start(bf16[16,2048]{1,0:T(8,128)(2,1)S(1)} %get-tuple-element.27), channel_id=1, source_target_pairs={{0,16},{8,24},{16,0},{24,8},{1,17},{9,25},{17,1},{25,9},{2,18},{10... | collective-permute-start | bytes 196616 | tf_op jit(solution)/shard_map/ppermute | solution.py:28
  22.0 6.1 %collective-permute-start.6 = (bf16[16,2048]{1,0:T(8,128)(2,1)S(1)}, bf16[16,2048]{1,0:T(8,128)(2,1)S(1)}, u32[]{:S(2)}, u32[]{:S(2)}) collective-permute-start(bf16[16,2048]{1,0:T(8,128)(2,1)S(1)} %get-tuple-element.28), channel_id=1, source_target_pairs={{0,24},{8,16},{16,8},{24,0},{1,25},{9,17},{17,9},{25,1},{2,26},{10... | collective-permute-start | bytes 196616 | tf_op jit(solution)/shard_map/ppermute | solution.py:28
  28.2 4.5 %collective-permute-start.7 = (bf16[16,1024]{1,0:T(8,128)(2,1)S(1)}, bf16[16,1024]{1,0:T(8,128)(2,1)S(1)}, u32[]{:S(2)}, u32[]{:S(2)}) collective-permute-start(bf16[16,1024]{1,0:T(8,128)(2,1)S(1)} %act.1.rest_0_), channel_id=1, source_target_pairs={{0,8},{8,0},{16,24},{24,16},{1,9},{9,1},{17,25},{25,17},{2,10},{10... | collective-permute-start | bytes 98312 | tf_op jit(solution)/shard_map/ppermute | solution.py:28
  29.5 5.4 %collective-permute-start.8 = (bf16[16,1024]{1,0:T(8,128)(2,1)S(1)}, bf16[16,1024]{1,0:T(8,128)(2,1)S(1)}, u32[]{:S(2)}, u32[]{:S(2)}) collective-permute-start(bf16[16,1024]{1,0:T(8,128)(2,1)S(1)} %act.1.rest_0_), channel_id=1, source_target_pairs={{0,16},{8,24},{16,0},{24,8},{1,17},{9,25},{17,1},{25,9},{2,18},{10... | collective-permute-start | bytes 98312 | tf_op jit(solution)/shard_map/ppermute | solution.py:28
  31.3 5.7 %collective-permute-start.9 = (bf16[16,1024]{1,0:T(8,128)(2,1)S(1)}, bf16[16,1024]{1,0:T(8,128)(2,1)S(1)}, u32[]{:S(2)}, u32[]{:S(2)}) collective-permute-start(bf16[16,1024]{1,0:T(8,128)(2,1)S(1)} %act.1.rest_0_), channel_id=1, source_target_pairs={{0,24},{8,16},{16,8},{24,0},{1,25},{9,17},{17,9},{25,1},{2,26},{10... | collective-permute-start | bytes 98312 | tf_op jit(solution)/shard_map/ppermute | solution.py:28
  37.8 1.6 %collective-permute-start.10 = (bf16[64,2048]{1,0:T(8,128)(2,1)S(1)}, bf16[64,2048]{1,0:T(8,128)(2,1)S(1)}, u32[]{:S(2)}, u32[]{:S(2)}) collective-permute-start(bf16[64,2048]{1,0:T(8,128)(2,1)S(1)} %down1.1), channel_id=1, source_target_pairs={{0,1},{1,0},{2,3},{3,2},{4,5},{5,4},{6,7},{7,6},{8,9},{9,8},{10,11... | collective-permute-start | bytes 786440 | tf_op jit(solution)/shard_map/ppermute | solution.py:28
  39.5 5.8 %collective-permute-start.13 = (bf16[16,2048]{1,0:T(8,128)(2,1)S(1)}, bf16[16,2048]{1,0:T(8,128)(2,1)S(1)}, u32[]{:S(2)}, u32[]{:S(2)}) collective-permute-start(bf16[16,2048]{1,0:T(8,128)(2,1)S(1)} %get-tuple-element.32), channel_id=1, source_target_pairs={{0,6},{1,7},{2,4},{3,5},{4,2},{5,3},{6,0},{7,1},{8,14},{9,15},{10,... | collective-permute-start | bytes 196616 | tf_op jit(solution)/shard_map/ppermute | solution.py:28
  40.1 5.3 %collective-permute-start.12 = (bf16[16,2048]{1,0:T(8,128)(2,1)S(1)}, bf16[16,2048]{1,0:T(8,128)(2,1)S(1)}, u32[]{:S(2)}, u32[]{:S(2)}) collective-permute-start(bf16[16,2048]{1,0:T(8,128)(2,1)S(1)} %get-tuple-element.33), channel_id=1, source_target_pairs={{0,4},{1,5},{2,6},{3,7},{4,0},{5,1},{6,2},{7,3},{8,12},{9,13},{10,... | collective-permute-start | bytes 196616 | tf_op jit(solution)/shard_map/ppermute | solution.py:28
  41.6 4.3 %collective-permute-start.11 = (bf16[16,2048]{1,0:T(8,128)(2,1)S(1)}, bf16[16,2048]{1,0:T(8,128)(2,1)S(1)}, u32[]{:S(2)}, u32[]{:S(2)}) collective-permute-start(bf16[16,2048]{1,0:T(8,128)(2,1)S(1)} %get-tuple-element.31), channel_id=1, source_target_pairs={{0,2},{1,3},{2,0},{3,1},{4,6},{5,7},{6,4},{7,5},{8,10},{9,11},{10,... | collective-permute-start | bytes 196616 | tf_op jit(solution)/shard_map/ppermute | solution.py:28

commit v3 on v2

--- a/solution.py
+++ b/solution.py
@@ -29,17 +29,26 @@
 
 
 def route_kernel(
-    cold_at, cold_ids, hot_ids, mask, *rest, order, rows, cold_blocks, hot_blocks, weights
+    cold_at, cold_ids_in, hot_ids_in, mask_in, *rest, order, rows, cold_blocks, hot_blocks, weights
 ):
     sources = rest[:weights]
     pick, spread, row_bits, bits = rest[weights : weights + 4]
     targets = rest[weights + 4 : 2 * weights + 4]
-    ordered, sems = rest[2 * weights + 4 :]
+    ordered, mask, turned, cold_ids, hot_ids, sems = rest[2 * weights + 4 :]
+    tables = ((mask_in, turned), (cold_ids_in, cold_ids), (hot_ids_in, hot_ids))
+    early = [
+        pltpu.make_async_copy(a, b, sems.at[weights + n]) for n, (a, b) in enumerate(tables)
+    ]
+    for copy in early:
+        copy.start()
     copies = [
         pltpu.make_async_copy(a, b, sems.at[n]) for n, (a, b) in enumerate(zip(sources, targets))
     ]
     for copy in copies:
         copy.start()
+    for copy in early:
+        copy.wait()
+    mask[...] = turned[...].T
     total, named = mask.shape
     own = cold_at[0]
     for at, mark in enumerate(order):
@@ -180,6 +189,8 @@
 
     weights = (hot_gate, hot_up, cold_gate, cold_up)
     weights = tuple(pltpu.with_memory_space_constraint(item, pltpu.HBM) for item in weights)
+    tables = (cold_ids, hot_ids, block_mask.T)
+    tables = tuple(pltpu.with_memory_space_constraint(item, pltpu.HBM) for item in tables)
     routed = pl.pallas_call(
         functools.partial(
             route_kernel,
@@ -196,16 +207,20 @@
             jax.ShapeDtypeStruct((total, bits_width), F32),
             *(jax.ShapeDtypeStruct(weight.shape, weight.dtype) for weight in weights),
         ),
-        in_specs=[SM, SM, SM, VM] + [HB] * len(weights),
+        in_specs=[SM, HB, HB, HB] + [HB] * len(weights),
         out_specs=(VM,) * (4 + len(weights)),
         scratch_shapes=[
             pltpu.VMEM((total, named), jnp.int32),
-            pltpu.SemaphoreType.DMA((len(weights),)),
+            pltpu.VMEM((total, named), jnp.int32),
+            pltpu.VMEM((named, total), jnp.int32),
+            pltpu.SMEM(cold_ids.shape, jnp.int32),
+            pltpu.SMEM(hot_ids.shape, jnp.int32),
+            pltpu.SemaphoreType.DMA((len(weights) + 3,)),
         ],
         compiler_params=params(24),
         cost_estimate=cost(50_000_000),
         name="route",
-    )(cold_at, cold_ids, hot_ids, block_mask, *weights)
+    )(cold_at, *tables, *weights)
     pick, spread, row_bits, bits = routed[:4]
 
     partial_sums = pl.pallas_call(

time: 46.8 us -> 43.8 us (0.936)
  local copies, waits for them, and re-layouts: 3.1 us -> 0.95 us
  Pallas kernels: 7.49 us -> 6.83 us
    unnamed x12 -> x7, local copies, waits for them, and re-layouts: 3.08 us -> 0.93 us
    pallas_call x1, Pallas kernels: 3.92 us -> 3.26 us  [body(): pl.pallas_call(functools.partial(route_kernel, order=order, rows=rows, co...]
  transfers between devices with their start and end apart: 14 -> 14, of which waited for: 11 -> 11; matrix products, arithmetic and copies ran while one was open for 4% -> 2% of each run, Pallas kernels for 10% -> 9%
where the time goes in v3:
time: 43.8 us; the launch traced here: 43.7 us
  waiting for transfers between devices  18 us (41%)
  starting transfers between devices  17 us (39%)
  Pallas kernels  6.83 us (16%)
  local copies, waits for them, and re-layouts  0.95 us (2%)
  other arithmetic  0.72 us (2%)
    ppermute x14, waiting for transfers between devices, send(): return lax.ppermute(value, axis, [(at, at ^ mask) for at in range(size)])  18 us
    ppermute x14, starting transfers between devices, send(): return lax.ppermute(value, axis, [(at, at ^ mask) for at in range(size)])  17 us
    pallas_call x1, Pallas kernels, body(): pl.pallas_call(functools.partial(route_kernel, order=order, rows=rows, co...  3.26 us
    pallas_call x1, Pallas kernels, body(): pl.pallas_call(functools.partial(up_kernel, parts=ranges), out_shape=tupl...  1.77 us
    pallas_call x2, Pallas kernels, down(): pl.pallas_call(functools.partial(down_kernel, parts=ranges, side=side), o...  1.7 us
    unnamed x7, local copies, waits for them, and re-layouts  0.93 us
  transfers between devices with their start and end apart: 14, of which 11 were waited for; matrix products, arithmetic and copies ran while one was open for 2% of the time, Pallas kernels for 9%

profile of v3, /device:TPU:0, one launch (start us, length us, event | category | flops | bytes accessed | tf_op | source)
XLA Modules:
  0.0 43.7 jit_solution(3079101229780921716)
XLA Ops:
  0.0 3.0 %collective-permute-start = (bf16[16,2048]{1,0:T(8,128)(2,1)}, bf16[16,2048]{1,0:T(8,128)(2,1)S(1)}, u32[]{:S(2)}, u32[]{:S(2)}) collective-permute-start(bf16[16,2048]{1,0:T(8,128)(2,1)} %param.10), channel_id=1, source_target_pairs={{0,2},{1,3},{2,0},{3,1},{4,6},{5,7},{6,4},{7,5},{8,10},{9,11},{10,... | collective-permute-start | bytes 196616 | tf_op jit(solution)/shard_map/ppermute | solution.py:28
  3.0 1.5 %collective-permute-start.1 = (bf16[16,2048]{1,0:T(8,128)(2,1)}, bf16[16,2048]{1,0:T(8,128)(2,1)S(1)}, u32[]{:S(2)}, u32[]{:S(2)}) collective-permute-start(bf16[16,2048]{1,0:T(8,128)(2,1)} %param.10), channel_id=1, source_target_pairs={{0,4},{1,5},{2,6},{3,7},{4,0},{5,1},{6,2},{7,3},{8,12},{9,13},{10,... | collective-permute-start | bytes 196616 | tf_op jit(solution)/shard_map/ppermute | solution.py:28
  4.5 0.0 collective-permute-start.2
  4.5 0.9 %constant_dynamic-update-slice_fusion.3 = bf16[64,2048]{1,0:T(8,128)(2,1)S(1)} fusion(bf16[16,2048]{1,0:T(8,128)(2,1)} %param.10), kind=kLoop, calls=%fused_computation.8 | loop fusion | bytes 131072
  5.4 0.2 collective-permute-done
  5.6 1.8 %collective-permute-done.1 = bf16[16,2048]{1,0:T(8,128)(2,1)S(1)} collective-permute-done((bf16[16,2048]{1,0:T(8,128)(2,1)}, bf16[16,2048]{1,0:T(8,128)(2,1)S(1)}, u32[]{:S(2)}, u32[]{:S(2)}) %collective-permute-start.1) | collective-permute-done | bytes 65568 | tf_op jit(solution)/shard_map/ppermute | solution.py:28
  7.5 2.4 %collective-permute-done.2 = bf16[16,2048]{1,0:T(8,128)(2,1)S(1)} collective-permute-done((bf16[16,2048]{1,0:T(8,128)(2,1)}, bf16[16,2048]{1,0:T(8,128)(2,1)S(1)}, u32[]{:S(2)}, u32[]{:S(2)}) %collective-permute-start.2) | collective-permute-done | bytes 65568 | tf_op jit(solution)/shard_map/ppermute | solution.py:28
  9.9 0.0 collective-permute-start.3
  9.9 3.3 %route.1 = (bf16[64,128]{1,0:T(8,128)(2,1)S(1)}, bf16[128,64]{1,0:T(8,128)(2,1)S(1)}, f32[64,8]{1,0:T(8,128)S(1)}, f32[128,8]{1,0:T(8,128)S(1)}, bf16[2048,128]{...) custom-call(s32[1]{0:T(128)} %bitcast.1.cold_at, ...), custom_call_target="tpu_custom_call" | custom-call | flops 50000000 | tf_op jit(solution)/shard_map/route/pallas_call | solution.py:194
  13.2 0.0 collective-permute-done.3.far
  13.2 0.0 copy-start
  13.2 0.0 copy-start.1
  13.2 1.8 %up.1 = (f32[16,2048]{1,0:T(8,128)S(1)}, bf16[16,2048]{1,0:T(8,128)(2,1)S(1)}, bf16[16,2048]{1,0:T(8,128)(2,1)S(1)}, bf16[16,2048]{1,0:T(8,128)(2,1)S(1)}) custom-call(s32[1]{0:T(128)} %bitcast.hot_at, bf16[64,2048]{1,0:T(8,128)(2,1)S(1)} %constant_dynamic-update-slice_fusion.near, bf16[64,2048]{1,0:T(8,128)(2,1)S(1)} %collective-permute-done.3.far, ...), custom_call_target="tpu_custom_call" | custom-call | tf_op jit(solution)/shard_map/up/pallas_call | solution.py:226
  15.0 1.6 %collective-permute-start.4 = (bf16[16,2048]{1,0:T(8,128)(2,1)S(1)}, bf16[16,2048]{1,0:T(8,128)(2,1)S(1)}, u32[]{:S(2)}, u32[]{:S(2)}) collective-permute-start(bf16[16,2048]{1,0:T(8,128)(2,1)S(1)} %get-tuple-element.26), channel_id=1, source_target_pairs={{0,8},{8,0},{16,24},{24,16},{1,9},{9,1},{17,25},{25,17},{2,10},{10... | collective-permute-start | bytes 196616 | tf_op jit(solution)/shard_map/ppermute | solution.py:28
  16.6 2.6 %collective-permute-start.5 = (bf16[16,2048]{1,0:T(8,128)(2,1)S(1)}, bf16[16,2048]{1,0:T(8,128)(2,1)S(1)}, u32[]{:S(2)}, u32[]{:S(2)}) collective-permute-start(bf16[16,2048]{1,0:T(8,128)(2,1)S(1)} %get-tuple-element.27), channel_id=1, source_target_pairs={{0,16},{8,24},{16,0},{24,8},{1,17},{9,25},{17,1},{25,9},{2,18},{10... | collective-permute-start | bytes 196616 | tf_op jit(solution)/shard_map/ppermute | solution.py:28
  19.2 0.2 collective-permute-start.6
  19.4 0.1 collective-permute-done.4.rest_1_
  19.5 4.1 %collective-permute-done.5.rest_2_ = bf16[16,2048]{1,0:T(8,128)(2,1)S(1)} collective-permute-done((bf16[16,2048]{1,0:T(8,128)(2,1)S(1)}, bf16[16,2048]{1,0:T(8,128)(2,1)S(1)}, u32[]{:S(2)}, u32[]{:S(2)}) %collective-permute-start.5) | collective-permute-done | bytes 65568 | tf_op jit(solution)/shard_map/ppermute | solution.py:28
  23.6 1.6 %collective-permute-done.6.rest_3_ = bf16[16,2048]{1,0:T(8,128)(2,1)S(1)} collective-permute-done((bf16[16,2048]{1,0:T(8,128)(2,1)S(1)}, bf16[16,2048]{1,0:T(8,128)(2,1)S(1)}, u32[]{:S(2)}, u32[]{:S(2)}) %collective-permute-start.6) | collective-permute-done | bytes 65568 | tf_op jit(solution)/shard_map/ppermute | solution.py:28
  25.3 0.1 act.1.rest_0_
  25.4 1.4 %collective-permute-start.7 = (bf16[16,1024]{1,0:T(8,128)(2,1)S(1)}, bf16[16,1024]{1,0:T(8,128)(2,1)S(1)}, u32[]{:S(2)}, u32[]{:S(2)}) collective-permute-start(bf16[16,1024]{1,0:T(8,128)(2,1)S(1)} %act.1.rest_0_), channel_id=1, source_target_pairs={{0,8},{8,0},{16,24},{24,16},{1,9},{9,1},{17,25},{25,17},{2,10},{10... | collective-permute-start | bytes 98312 | tf_op jit(solution)/shard_map/ppermute | solution.py:28
  26.7 1.7 %collective-permute-start.8 = (bf16[16,1024]{1,0:T(8,128)(2,1)S(1)}, bf16[16,1024]{1,0:T(8,128)(2,1)S(1)}, u32[]{:S(2)}, u32[]{:S(2)}) collective-permute-start(bf16[16,1024]{1,0:T(8,128)(2,1)S(1)} %act.1.rest_0_), channel_id=1, source_target_pairs={{0,16},{8,24},{16,0},{24,8},{1,17},{9,25},{17,1},{25,9},{2,18},{10... | collective-permute-start | bytes 98312 | tf_op jit(solution)/shard_map/ppermute | solution.py:28
  28.4 1.4 %collective-permute-start.9 = (bf16[16,1024]{1,0:T(8,128)(2,1)S(1)}, bf16[16,1024]{1,0:T(8,128)(2,1)S(1)}, u32[]{:S(2)}, u32[]{:S(2)}) collective-permute-start(bf16[16,1024]{1,0:T(8,128)(2,1)S(1)} %act.1.rest_0_), channel_id=1, source_target_pairs={{0,24},{8,16},{16,8},{24,0},{1,25},{9,17},{17,9},{25,1},{2,26},{10... | collective-permute-start | bytes 98312 | tf_op jit(solution)/shard_map/ppermute | solution.py:28
  29.8 0.0 collective-permute-done.7.rest_1_
  29.8 2.3 %collective-permute-done.8.rest_2_ = bf16[16,1024]{1,0:T(8,128)(2,1)S(1)} collective-permute-done((bf16[16,1024]{1,0:T(8,128)(2,1)S(1)}, bf16[16,1024]{1,0:T(8,128)(2,1)S(1)}, u32[]{:S(2)}, u32[]{:S(2)}) %collective-permute-start.8) | collective-permute-done | bytes 32800 | tf_op jit(solution)/shard_map/ppermute | solution.py:28
  32.1 2.1 %collective-permute-done.9.rest_3_ = bf16[16,1024]{1,0:T(8,128)(2,1)S(1)} collective-permute-done((bf16[16,1024]{1,0:T(8,128)(2,1)S(1)}, bf16[16,1024]{1,0:T(8,128)(2,1)S(1)}, u32[]{:S(2)}, u32[]{:S(2)}) %collective-permute-start.9) | collective-permute-done | bytes 32800 | tf_op jit(solution)/shard_map/ppermute | solution.py:28
  34.1 0.0 copy-done
  34.2 0.0 copy-done.1
  34.2 0.9 %down1.1 = bf16[64,2048]{1,0:T(8,128)(2,1)S(1)} custom-call(s32[1]{0:T(128)} %bitcast.hot_at, bf16[128,64]{1,0:T(8,128)(2,1)S(1)} %get-tuple-element.17.spread, bf16[768,2048]{1,0:T(8,128)(2,1)S(1)} %copy-done, bf16[128,2048]{1,0:T(8,128)(2,1)S(1)} %copy-done.1, bf16[16,1024]{1,0:T(8,128)(2,1)S(1)} %act.1.rest_0_, ...), custom_call_target="tpu_custom_call" | custom-call | flops 20000000 | tf_op jit(solution)/shard_map/down1/pallas_call | solution.py:252
  35.0 0.1 collective-permute-start.10
  35.1 0.9 %down0.1 = f32[64,2048]{1,0:T(8,128)S(1)} custom-call(s32[1]{0:T(128)} %bitcast.hot_at, bf16[128,64]{1,0:T(8,128)(2,1)S(1)} %get-tuple-element.17.spread, bf16[768,2048]{1,0:T(8,128)(2,1)S(1)} %copy-done, bf16[128,2048]{1,0:T(8,128)(2,1)S(1)} %copy-done.1, bf16[16,1024]{1,0:T(8,128)(2,1)S(1)} %act.1.rest_0_, ...), custom_call_target="tpu_custom_call" | custom-call | flops 20000000 | tf_op jit(solution)/shard_map/down0/pallas_call | solution.py:252
  35.9 0.7 %collective-permute-done.10 = bf16[64,2048]{1,0:T(8,128)(2,1)S(1)} collective-permute-done((bf16[64,2048]{1,0:T(8,128)(2,1)S(1)}, bf16[64,2048]{1,0:T(8,128)(2,1)S(1)}, u32[]{:S(2)}, u32[]{:S(2)}) %collective-permute-start.10) | collective-permute-done | bytes 262176 | tf_op jit(solution)/shard_map/ppermute | solution.py:28
  36.6 0.1 fusion.3
  36.7 0.5 %collective-permute-start.13 = (bf16[16,2048]{1,0:T(8,128)(2,1)S(1)}, bf16[16,2048]{1,0:T(8,128)(2,1)S(1)}, u32[]{:S(2)}, u32[]{:S(2)}) collective-permute-start(bf16[16,2048]{1,0:T(8,128)(2,1)S(1)} %get-tuple-element.32), channel_id=1, source_target_pairs={{0,6},{1,7},{2,4},{3,5},{4,2},{5,3},{6,0},{7,1},{8,14},{9,15},{10,... | collective-permute-start | bytes 196616 | tf_op jit(solution)/shard_map/ppermute | solution.py:28
  37.2 1.5 %collective-permute-start.12 = (bf16[16,2048]{1,0:T(8,128)(2,1)S(1)}, bf16[16,2048]{1,0:T(8,128)(2,1)S(1)}, u32[]{:S(2)}, u32[]{:S(2)}) collective-permute-start(bf16[16,2048]{1,0:T(8,128)(2,1)S(1)} %get-tuple-element.33), channel_id=1, source_target_pairs={{0,4},{1,5},{2,6},{3,7},{4,0},{5,1},{6,2},{7,3},{8,12},{9,13},{10,... | collective-permute-start | bytes 196616 | tf_op jit(solution)/shard_map/ppermute | solution.py:28
  38.7 1.5 %collective-permute-start.11 = (bf16[16,2048]{1,0:T(8,128)(2,1)S(1)}, bf16[16,2048]{1,0:T(8,128)(2,1)S(1)}, u32[]{:S(2)}, u32[]{:S(2)}) collective-permute-start(bf16[16,2048]{1,0:T(8,128)(2,1)S(1)} %get-tuple-element.31), channel_id=1, source_target_pairs={{0,2},{1,3},{2,0},{3,1},{4,6},{5,7},{6,4},{7,5},{8,10},{9,11},{10,... | collective-permute-start | bytes 196616 | tf_op jit(solution)/shard_map/ppermute | solution.py:28
  40.3 2.2 %collective-permute-done.13 = bf16[16,2048]{1,0:T(8,128)(2,1)S(1)} collective-permute-done((bf16[16,2048]{1,0:T(8,128)(2,1)S(1)}, bf16[16,2048]{1,0:T(8,128)(2,1)S(1)}, u32[]{:S(2)}, u32[]{:S(2)}) %collective-permute-start.13) | collective-permute-done | bytes 65568 | tf_op jit(solution)/shard_map/ppermute | solution.py:28
  42.5 0.0 collective-permute-done.12
  42.5 0.5 %collective-permute-done.11 = bf16[16,2048]{1,0:T(8,128)(2,1)S(1)} collective-permute-done((bf16[16,2048]{1,0:T(8,128)(2,1)S(1)}, bf16[16,2048]{1,0:T(8,128)(2,1)S(1)}, u32[]{:S(2)}, u32[]{:S(2)}) %collective-permute-start.11) | collective-permute-done | bytes 65568 | tf_op jit(solution)/shard_map/ppermute | solution.py:28
  43.0 0.7 %fusion.2 = bf16[16,2048]{1,0:T(8,128)(2,1)} fusion(f32[64,2048]{1,0:T(8,128)S(1)} %get-tuple-element.30, bf16[16,2048]{1,0:T(8,128)(2,1)S(1)} %collective-permute-done.13, bf16[16,2048]{1,0:T(8,128)(2,1)S(1)} %collective-permute-done.12, bf16[16,2048]{1,0:T(8,128)(2,1)S(1)} %collective-permute-done.11), kind=kLoop, calls=%fused_computation.4 | loop fusion | flops 229376 | bytes 393216 | tf_op jit(solution)/shard_map/convert_element_type | solution.py:269
  (4 shorter events, 0.0 us)
Async XLA Ops:
  0.0 5.6 %collective-permute-start = (bf16[16,2048]{1,0:T(8,128)(2,1)}, bf16[16,2048]{1,0:T(8,128)(2,1)S(1)}, u32[]{:S(2)}, u32[]{:S(2)}) collective-permute-start(bf16[16,2048]{1,0:T(8,128)(2,1)} %param.10), channel_id=1, source_target_pairs={{0,2},{1,3},{2,0},{3,1},{4,6},{5,7},{6,4},{7,5},{8,10},{9,11},{10,... | collective-permute-start | bytes 196616 | tf_op jit(solution)/shard_map/ppermute | solution.py:28
  3.0 4.5 %collective-permute-start.1 = (bf16[16,2048]{1,0:T(8,128)(2,1)}, bf16[16,2048]{1,0:T(8,128)(2,1)S(1)}, u32[]{:S(2)}, u32[]{:S(2)}) collective-permute-start(bf16[16,2048]{1,0:T(8,128)(2,1)} %param.10), channel_id=1, source_target_pairs={{0,4},{1,5},{2,6},{3,7},{4,0},{5,1},{6,2},{7,3},{8,12},{9,13},{10,... | collective-permute-start | bytes 196616 | tf_op jit(solution)/shard_map/ppermute | solution.py:28
  4.5 5.4 %collective-permute-start.2 = (bf16[16,2048]{1,0:T(8,128)(2,1)}, bf16[16,2048]{1,0:T(8,128)(2,1)S(1)}, u32[]{:S(2)}, u32[]{:S(2)}) collective-permute-start(bf16[16,2048]{1,0:T(8,128)(2,1)} %param.10), channel_id=1, source_target_pairs={{0,6},{1,7},{2,4},{3,5},{4,2},{5,3},{6,0},{7,1},{8,14},{9,15},{10,... | collective-permute-start | bytes 196616 | tf_op jit(solution)/shard_map/ppermute | solution.py:28
  9.9 3.3 %collective-permute-start.3 = (bf16[64,2048]{1,0:T(8,128)(2,1)S(1)}, bf16[64,2048]{1,0:T(8,128)(2,1)S(1)}, u32[]{:S(2)}, u32[]{:S(2)}) collective-permute-start(bf16[64,2048]{1,0:T(8,128)(2,1)S(1)} %constant_dynamic-update-slice_fusion.near), channel_id=1, source_target_pairs={{0,1},{1,0},{2,3},{3,2},{4,5},{5,4},{6,7},{7,6},{8,9},{9,8},{10,11... | collective-permute-start | bytes 786440 | tf_op jit(solution)/shard_map/ppermute | solution.py:28
  13.2 21.0 %copy-start = (bf16[768,2048]{1,0:T(8,128)(2,1)S(1)}, bf16[768,2048]{1,0:T(8,128)(2,1)}, u32[]{:S(2)}) copy-start(bf16[768,2048]{1,0:T(8,128)(2,1)} %cold_down.3) | copy-start | bytes 9437188
  13.2 21.0 %copy-start.1 = (bf16[128,2048]{1,0:T(8,128)(2,1)S(1)}, bf16[128,2048]{1,0:T(8,128)(2,1)}, u32[]{:S(2)}) copy-start(bf16[128,2048]{1,0:T(8,128)(2,1)} %hot_down.3) | copy-start | bytes 1572868
  15.0 4.6 %collective-permute-start.4 = (bf16[16,2048]{1,0:T(8,128)(2,1)S(1)}, bf16[16,2048]{1,0:T(8,128)(2,1)S(1)}, u32[]{:S(2)}, u32[]{:S(2)}) collective-permute-start(bf16[16,2048]{1,0:T(8,128)(2,1)S(1)} %get-tuple-element.26), channel_id=1, source_target_pairs={{0,8},{8,0},{16,24},{24,16},{1,9},{9,1},{17,25},{25,17},{2,10},{10... | collective-permute-start | bytes 196616 | tf_op jit(solution)/shard_map/ppermute | solution.py:28
  16.6 7.0 %collective-permute-start.5 = (bf16[16,2048]{1,0:T(8,128)(2,1)S(1)}, bf16[16,2048]{1,0:T(8,128)(2,1)S(1)}, u32[]{:S(2)}, u32[]{:S(2)}) collective-permute-start(bf16[16,2048]{1,0:T(8,128)(2,1)S(1)} %get-tuple-element.27), channel_id=1, source_target_pairs={{0,16},{8,24},{16,0},{24,8},{1,17},{9,25},{17,1},{25,9},{2,18},{10... | collective-permute-start | bytes 196616 | tf_op jit(solution)/shard_map/ppermute | solution.py:28
  19.2 6.1 %collective-permute-start.6 = (bf16[16,2048]{1,0:T(8,128)(2,1)S(1)}, bf16[16,2048]{1,0:T(8,128)(2,1)S(1)}, u32[]{:S(2)}, u32[]{:S(2)}) collective-permute-start(bf16[16,2048]{1,0:T(8,128)(2,1)S(1)} %get-tuple-element.28), channel_id=1, source_target_pairs={{0,24},{8,16},{16,8},{24,0},{1,25},{9,17},{17,9},{25,1},{2,26},{10... | collective-permute-start | bytes 196616 | tf_op jit(solution)/shard_map/ppermute | solution.py:28
  25.4 4.5 %collective-permute-start.7 = (bf16[16,1024]{1,0:T(8,128)(2,1)S(1)}, bf16[16,1024]{1,0:T(8,128)(2,1)S(1)}, u32[]{:S(2)}, u32[]{:S(2)}) collective-permute-start(bf16[16,1024]{1,0:T(8,128)(2,1)S(1)} %act.1.rest_0_), channel_id=1, source_target_pairs={{0,8},{8,0},{16,24},{24,16},{1,9},{9,1},{17,25},{25,17},{2,10},{10... | collective-permute-start | bytes 98312 | tf_op jit(solution)/shard_map/ppermute | solution.py:28
  26.7 5.4 %collective-permute-start.8 = (bf16[16,1024]{1,0:T(8,128)(2,1)S(1)}, bf16[16,1024]{1,0:T(8,128)(2,1)S(1)}, u32[]{:S(2)}, u32[]{:S(2)}) collective-permute-start(bf16[16,1024]{1,0:T(8,128)(2,1)S(1)} %act.1.rest_0_), channel_id=1, source_target_pairs={{0,16},{8,24},{16,0},{24,8},{1,17},{9,25},{17,1},{25,9},{2,18},{10... | collective-permute-start | bytes 98312 | tf_op jit(solution)/shard_map/ppermute | solution.py:28
  28.4 5.7 %collective-permute-start.9 = (bf16[16,1024]{1,0:T(8,128)(2,1)S(1)}, bf16[16,1024]{1,0:T(8,128)(2,1)S(1)}, u32[]{:S(2)}, u32[]{:S(2)}) collective-permute-start(bf16[16,1024]{1,0:T(8,128)(2,1)S(1)} %act.1.rest_0_), channel_id=1, source_target_pairs={{0,24},{8,16},{16,8},{24,0},{1,25},{9,17},{17,9},{25,1},{2,26},{10... | collective-permute-start | bytes 98312 | tf_op jit(solution)/shard_map/ppermute | solution.py:28
  35.0 1.6 %collective-permute-start.10 = (bf16[64,2048]{1,0:T(8,128)(2,1)S(1)}, bf16[64,2048]{1,0:T(8,128)(2,1)S(1)}, u32[]{:S(2)}, u32[]{:S(2)}) collective-permute-start(bf16[64,2048]{1,0:T(8,128)(2,1)S(1)} %down1.1), channel_id=1, source_target_pairs={{0,1},{1,0},{2,3},{3,2},{4,5},{5,4},{6,7},{7,6},{8,9},{9,8},{10,11... | collective-permute-start | bytes 786440 | tf_op jit(solution)/shard_map/ppermute | solution.py:28
  36.7 5.8 %collective-permute-start.13 = (bf16[16,2048]{1,0:T(8,128)(2,1)S(1)}, bf16[16,2048]{1,0:T(8,128)(2,1)S(1)}, u32[]{:S(2)}, u32[]{:S(2)}) collective-permute-start(bf16[16,2048]{1,0:T(8,128)(2,1)S(1)} %get-tuple-element.32), channel_id=1, source_target_pairs={{0,6},{1,7},{2,4},{3,5},{4,2},{5,3},{6,0},{7,1},{8,14},{9,15},{10,... | collective-permute-start | bytes 196616 | tf_op jit(solution)/shard_map/ppermute | solution.py:28
  37.2 5.3 %collective-permute-start.12 = (bf16[16,2048]{1,0:T(8,128)(2,1)S(1)}, bf16[16,2048]{1,0:T(8,128)(2,1)S(1)}, u32[]{:S(2)}, u32[]{:S(2)}) collective-permute-start(bf16[16,2048]{1,0:T(8,128)(2,1)S(1)} %get-tuple-element.33), channel_id=1, source_target_pairs={{0,4},{1,5},{2,6},{3,7},{4,0},{5,1},{6,2},{7,3},{8,12},{9,13},{10,... | collective-permute-start | bytes 196616 | tf_op jit(solution)/shard_map/ppermute | solution.py:28
  38.7 4.3 %collective-permute-start.11 = (bf16[16,2048]{1,0:T(8,128)(2,1)S(1)}, bf16[16,2048]{1,0:T(8,128)(2,1)S(1)}, u32[]{:S(2)}, u32[]{:S(2)}) collective-permute-start(bf16[16,2048]{1,0:T(8,128)(2,1)S(1)} %get-tuple-element.31), channel_id=1, source_target_pairs={{0,2},{1,3},{2,0},{3,1},{4,6},{5,7},{6,4},{7,5},{8,10},{9,11},{10,... | collective-permute-start | bytes 196616 | tf_op jit(solution)/shard_map/ppermute | solution.py:28
